TPU v7x, 32 devices: a whole 2x2x4 slice. The times are simulated.
32 devices in a mesh: expert: 4 (over z), shard: 8 (over y, x, core).
Axes of the slice: x: 2, y: 2, z: 4, core: 2. Of those that a mesh axis runs over, the one named last changes fastest.
Arguments:
- master_gate: float32 [64, 2048, 1408], P('expert', 'shard'), may hold values from -0.1875 to 0.1875
- master_up: float32 [64, 2048, 1408], P('expert', 'shard'), may hold values from -0.1875 to 0.1875
- router_weight: float32 [2048, 64], P('shard', 'expert'), may hold values from -0.125 to 0.125
- router_gain: float32 [2048], P('shard'), may hold values from 0.25 to 1.75
Outputs:
- final_gate: bfloat16 [64, 2048, 1408], P('expert', None, 'shard')
- final_up: bfloat16 [64, 2048, 1408], P('expert', None, 'shard')
- scale_gate: float32 [64, 1408], P('expert', 'shard')
- scale_up: float32 [64, 1408], P('expert', 'shard')
- serve_router: bfloat16 [2048, 64], replicated
All inputs are finite; a program needn't handle non-finite values.
Results may differ from a plain program's by a relative error of at most 0.001.
Values may be sent and summed in bfloat16 or wider, within the bound.
No kernel may reach another device: no remote copies, remote signals or barrier semaphores. Data moves between devices by JAX's collectives and lax.ppermute only.
A program may use at most 192 MiB of HBM per device.

v0:
```python
import jax
import jax.numpy as jnp
from jax import lax
from jax.sharding import PartitionSpec as P


def local(master_gate, master_up, router_weight, router_gain):
    total_gate, total_up = lax.psum(
        (jnp.sum(master_gate * master_gate, axis=1), jnp.sum(master_up * master_up, axis=1)),
        "shard",
    )
    scale_gate = jnp.sqrt(total_gate)
    scale_up = jnp.sqrt(total_up)
    narrow_gate, narrow_up = (
        (master_gate / jnp.expand_dims(scale_gate, 1)).astype(jnp.bfloat16),
        (master_up / jnp.expand_dims(scale_up, 1)).astype(jnp.bfloat16),
    )
    final_gate, final_up = (
        lax.all_to_all(narrow_gate, "shard", split_axis=2, concat_axis=1, tiled=True),
        lax.all_to_all(narrow_up, "shard", split_axis=2, concat_axis=1, tiled=True),
    )
    scale_gate = lax.dynamic_slice_in_dim(
        scale_gate, lax.axis_index("shard") * final_gate.shape[2], final_gate.shape[2], axis=1
    )
    scale_up = lax.dynamic_slice_in_dim(
        scale_up, lax.axis_index("shard") * final_up.shape[2], final_up.shape[2], axis=1
    )
    part_router = (router_weight * router_gain[:, None]).astype(jnp.bfloat16)
    row_router = lax.all_gather(part_router, "shard", axis=0, tiled=True)
    serve_router = lax.all_gather(row_router, "expert", axis=1, tiled=True)
    return (final_gate, final_up, scale_gate, scale_up, serve_router)


def solution(mesh):
    in_specs = (
        P("expert", "shard", None),
        P("expert", "shard", None),
        P("shard", "expert"),
        P("shard"),
    )
    out_specs = (
        P("expert", None, "shard"),
        P("expert", None, "shard"),
        P("expert", "shard"),
        P("expert", "shard"),
        P(),
    )
    return jax.shard_map(local, mesh=mesh, in_specs=in_specs, out_specs=out_specs, check_vma=False)
```

profile of v0, /device:TPU:0, one launch (start us, length us, event | category | flops | bytes accessed | tf_op | source)
XLA Modules:
  0.0 445.2 jit_solution(13781813590717320649)
XLA Ops:
  7.2 0.0 all-reduce.3.cloned.1.call-start
  7.2 15.8 %multiply_reduce_fusion = (f32[16,1408]{1,0:T(8,128)}, f32[16,1408]{1,0:T(8,128)}) fusion(f32[16,256,1408]{2,1,0:T(8,128)} %param.5, f32[16,256,1408]{2,1,0:T(8,128)} %param.4), kind=kLoop, calls=%fused_computation.1 | loop fusion | flops 23023616 | bytes 46317568 | tf_op jit(solution)/shard_map/reduce_sum | solution.py:9
  23.0 0.0 all-reduce.3.cloned.1.call-update
  23.1 23.7 %copy.22 = f32[16,256,1408]{1,0,2:T(8,128)} copy(f32[16,256,1408]{2,1,0:T(8,128)} %param.5) | data formatting | bytes 46137344 | tf_op args[1]
  46.8 32.3 %all-reduce.3.cloned.1.call-done = (f32[16,1408]{1,0:T(8,128)}, f32[16,1408]{1,0:T(8,128)}) async-done(((f32[16,1408]{1,0:T(8,128)}, f32[16,1408]{1,0:T(8,128)}), (f32[16,1408]{1,0:T(8,128)}, f32[16,1408]{1,0:T(8,128)})) %all-reduce.3.cloned.1.call-update) | async-done | bytes 180240 | tf_op jit(solution)/shard_map/psum | solution.py:8
  79.0 0.9 sqrt.7
  80.0 0.3 copy.21
  80.2 14.2 %divide_convert_fusion = bf16[16,256,1408]{1,0,2:T(8,128)(2,1)} fusion(f32[16,256,1408]{1,0,2:T(8,128)} %copy.22, f32[16,1408]{0,1:T(8,128)S(1)} %copy.21), kind=kLoop, calls=%fused_computation | loop fusion | flops 11534336 | bytes 34693120 | tf_op jit(solution)/shard_map/convert_element_type | solution.py:16
  94.4 5.2 %all-to-all-start.1 = ((bf16[16,256,1408]{1,0,2:T(8,128)(2,1)}), bf16[16,256,1408]{1,0,2:T(8,128)(2,1)}, u32[]{:S(2)}, u32[]{:S(2)}) async-start(bf16[16,256,1408]{1,0,2:T(8,128)(2,1)} %divide_convert_fusion), calls=%async_computation.1 | async-start | bytes 23068672 | tf_op jit(solution)/shard_map/all_to_all | solution.py:20
  99.7 0.0 copy-start
  99.7 23.7 %copy.18 = f32[16,256,1408]{1,0,2:T(8,128)} copy(f32[16,256,1408]{2,1,0:T(8,128)} %param.4) | data formatting | bytes 46137344 | tf_op args[0]
  123.4 0.0 copy-done
  123.4 0.3 copy.17
  123.7 0.0 copy-start.1
  123.7 0.0 copy-start.2
  123.7 14.2 %divide_convert_fusion.1 = bf16[16,256,1408]{1,0,2:T(8,128)(2,1)} fusion(f32[16,256,1408]{1,0,2:T(8,128)} %copy.18, f32[16,1408]{0,1:T(8,128)S(1)} %copy.17), kind=kLoop, calls=%fused_computation.2 | loop fusion | flops 11534336 | bytes 34693120 | tf_op jit(solution)/shard_map/convert_element_type | solution.py:15
  138.0 89.5 %all-to-all-done.1 = bf16[16,256,1408]{1,0,2:T(8,128)(2,1)} async-done(((bf16[16,256,1408]{1,0,2:T(8,128)(2,1)}), bf16[16,256,1408]{1,0,2:T(8,128)(2,1)}, u32[]{:S(2)}, u32[]{:S(2)}) %all-to-all-start.1) | async-done | bytes 11534368 | tf_op jit(solution)/shard_map/all_to_all | solution.py:20
  227.4 5.3 %all-to-all-start = ((bf16[16,256,1408]{1,0,2:T(8,128)(2,1)}), bf16[16,256,1408]{1,0,2:T(8,128)(2,1)}, u32[]{:S(2)}, u32[]{:S(2)}) async-start(bf16[16,256,1408]{1,0,2:T(8,128)(2,1)} %divide_convert_fusion.1), calls=%async_computation | async-start | bytes 23068672 | tf_op jit(solution)/shard_map/all_to_all | solution.py:19
  232.7 0.0 copy-done.1
  232.7 0.0 copy-done.2
  232.7 130.9 %all_gather.6 = bf16[2048,16]{0,1:T(8,128)(2,1)S(1)} all-gather(bf16[256,16]{0,1:T(8,128)(2,1)S(1)} %multiply_convert_fusion), channel_id=1, replica_groups=mesh['expert'=4,'shard'=8] {'shard'}, dimensions={0}, use_global_device_ids=true | all-gather | bytes 73728 | tf_op jit(solution)/shard_map/all_gather | solution.py:29
  363.6 14.0 %all_gather.7 = bf16[2048,64]{0,1:T(8,128)(2,1)S(1)} all-gather(bf16[2048,16]{0,1:T(8,128)(2,1)S(1)} %all_gather.6), channel_id=1, replica_groups=mesh['expert'=4,'shard'=8] {'expert'}, dimensions={1}, use_global_device_ids=true | all-gather | bytes 327680 | tf_op jit(solution)/shard_map/all_gather | solution.py:30
  377.6 0.7 constant_dynamic-slice_fusion
  378.3 0.7 constant_dynamic-slice_fusion.1
  379.0 11.4 %copy.24 = bf16[16,8,256,176]{2,1,3,0:T(8,128)(2,1)} copy(bf16[16,8,256,176]{2,0,3,1:T(8,128)(2,1)} %bitcast.5) | data formatting | bytes 23068672 | tf_op jit(solution)/shard_map/all_to_all | solution.py:20
  390.4 18.0 %all_to_all.33 = bf16[16,2048,176]{1,2,0:T(8,128)(2,1)} reshape(bf16[16,8,256,176]{2,1,3,0:T(8,128)(2,1)} %copy.24) | data formatting | bytes 23068672 | tf_op jit(solution)/shard_map/all_to_all | solution.py:20
  408.3 0.0 all-to-all-done
  408.3 11.4 %copy.20 = bf16[16,8,256,176]{2,1,3,0:T(8,128)(2,1)} copy(bf16[16,8,256,176]{2,0,3,1:T(8,128)(2,1)} %bitcast.2) | data formatting | bytes 23068672 | tf_op jit(solution)/shard_map/all_to_all | solution.py:19
  419.7 18.0 %all_to_all.29 = bf16[16,2048,176]{1,2,0:T(8,128)(2,1)} reshape(bf16[16,8,256,176]{2,1,3,0:T(8,128)(2,1)} %copy.20) | data formatting | bytes 23068672 | tf_op jit(solution)/shard_map/all_to_all | solution.py:19
  437.7 0.7 copy.30
  (2 shorter events, 0.0 us)
Async XLA Ops:
  7.2 71.9 %all-reduce.3.cloned.1.call-start = ((), (), s32[]{:S(2)}) async-start(), calls=%async_computation.2 | async-start | bytes 360448 | tf_op jit(solution)/shard_map/psum | solution.py:8
  94.4 133.0 %all-to-all-start.1 = ((bf16[16,256,1408]{1,0,2:T(8,128)(2,1)}), bf16[16,256,1408]{1,0,2:T(8,128)(2,1)}, u32[]{:S(2)}, u32[]{:S(2)}) async-start(bf16[16,256,1408]{1,0,2:T(8,128)(2,1)} %divide_convert_fusion), calls=%async_computation.1 | async-start | bytes 23068672 | tf_op jit(solution)/shard_map/all_to_all | solution.py:20
  99.7 23.7 %copy-start = (f32[16,1408]{1,0:T(8,128)S(1)}, f32[16,1408]{1,0:T(8,128)}, u32[]{:S(2)}) copy-start(f32[16,1408]{1,0:T(8,128)} %get-tuple-element.5) | copy-start | bytes 270340
  123.7 109.0 %copy-start.1 = (f32[256,16]{0,1:T(8,128)S(1)}, f32[256,16]{0,1:T(8,128)}, u32[]{:S(2)}) copy-start(f32[256,16]{0,1:T(8,128)} %param.6) | copy-start | bytes 49156
  123.7 109.0 %copy-start.2 = (f32[256]{0:T(256)S(1)}, f32[256]{0:T(256)}, u32[]{:S(2)}) copy-start(f32[256]{0:T(256)} %param.7) | copy-start | bytes 3076
  227.4 180.9 %all-to-all-start = ((bf16[16,256,1408]{1,0,2:T(8,128)(2,1)}), bf16[16,256,1408]{1,0,2:T(8,128)(2,1)}, u32[]{:S(2)}, u32[]{:S(2)}) async-start(bf16[16,256,1408]{1,0,2:T(8,128)(2,1)} %divide_convert_fusion.1), calls=%async_computation | async-start | bytes 23068672 | tf_op jit(solution)/shard_map/all_to_all | solution.py:19
Sparse Core Ops, SparseCore 0:
  23.2 55.8 all-reduce.2
where the time goes:
time: 447 us; the launch traced here: 445 us
  blocking collectives  145 us (32%)
  waiting for transfers between devices  122 us (27%)
  local copies, waits for them, and re-layouts  110 us (25%)
  other arithmetic  44.3 us (10%)
  between operations  14.1 us (3%)
  starting transfers between devices  10.5 us (2%)
    all_gather x1, blocking collectives, local(): row_router = lax.all_gather(part_router, 'shard', axis=0, tiled=True)  131 us
    all_to_all x1, waiting for transfers between devices, local(): lax.all_to_all(narrow_up, 'shard', split_axis=2, concat_axis=1, tiled=True)  89.5 us
    unnamed x9, local copies, waits for them, and re-layouts  48.1 us
    psum x1, waiting for transfers between devices, local(): lax.psum((jnp.sum(master_gate * master_gate, axis=1), jnp.sum(master_up *...  32.3 us
    all_to_all x2, local copies, waits for them, and re-layouts, local(): lax.all_to_all(narrow_gate, 'shard', split_axis=2, concat_axis=1, tiled=T...  29.3 us
    all_to_all x2, local copies, waits for them, and re-layouts, local(): lax.all_to_all(narrow_up, 'shard', split_axis=2, concat_axis=1, tiled=True)  29.3 us
    reduce_sum x1, other arithmetic, local(): jnp.sum(master_up * master_up, axis=1)  15.8 us
    convert_element_type x1, other arithmetic, local(): (master_up / jnp.expand_dims(scale_up, 1)).astype(jnp.bfloat16)  14.2 us
  transfers between devices with their start and end apart: 3, of which 2 were waited for; matrix products, arithmetic and copies ran while one was open for 17% of the time, Pallas kernels for 0%

commit v1 on v0

v1 whole, which is shorter than its diff:
```python
import jax
import jax.numpy as jnp
from jax import lax
from jax.experimental import pallas as pl
from jax.experimental.pallas import tpu as pltpu
from jax.sharding import PartitionSpec as P


SPAN = 248.0
HALF = 124.0
TINY = 1e-30
FAR = pl.BlockSpec(memory_space=pltpu.MemorySpace.HBM)


def plain(master_gate, master_up, router_weight, router_gain):
    total_gate, total_up = lax.psum(
        (jnp.sum(master_gate * master_gate, axis=1), jnp.sum(master_up * master_up, axis=1)),
        "shard",
    )
    scale_gate = jnp.sqrt(total_gate)
    scale_up = jnp.sqrt(total_up)
    narrow_gate = (master_gate / jnp.expand_dims(scale_gate, 1)).astype(jnp.bfloat16)
    narrow_up = (master_up / jnp.expand_dims(scale_up, 1)).astype(jnp.bfloat16)
    final_gate = lax.all_to_all(narrow_gate, "shard", split_axis=2, concat_axis=1, tiled=True)
    final_up = lax.all_to_all(narrow_up, "shard", split_axis=2, concat_axis=1, tiled=True)
    mine = lax.axis_index("shard") * final_gate.shape[2]
    scale_gate = lax.dynamic_slice_in_dim(scale_gate, mine, final_gate.shape[2], axis=1)
    scale_up = lax.dynamic_slice_in_dim(scale_up, mine, final_up.shape[2], axis=1)
    part_router = (router_weight * router_gain[:, None]).astype(jnp.bfloat16)
    row_router = lax.all_gather(part_router, "shard", axis=0, tiled=True)
    serve_router = lax.all_gather(row_router, "expert", axis=1, tiled=True)
    return (final_gate, final_up, scale_gate, scale_up, serve_router)


def column_max(x):
    return jnp.max(jnp.abs(x), axis=0, keepdims=True).astype(jnp.bfloat16).astype(jnp.float32)


def encode_kernel(n, piece, *refs):
    x_ref = refs[0]
    outs, turned = refs[-1 - n : -1], refs[-1]
    me = lax.axis_index("shard")
    x = x_ref[0]
    top = column_max(x)
    step = jnp.where(top > TINY, SPAN / jnp.maximum(top, TINY), 0.0)
    y = jnp.exp2(jnp.abs(x) * step - HALF)
    y = jnp.where(x < 0, -y, y)
    turned[...] = y.astype(jnp.bfloat16).T
    for o in range(n):
        first = pl.multiple_of((me ^ o) * piece, 16)
        outs[o][0] = turned[pl.ds(first, piece), :]


def encode(x, first, count, n, after=()):
    _, rows, cols = x.shape
    piece = cols // n
    block = jax.ShapeDtypeStruct((count, piece, rows), jnp.bfloat16)
    return pl.pallas_call(
        lambda *refs: encode_kernel(n, piece, *refs),
        name="encode",
        grid=(count,),
        out_shape=[block] * n,
        in_specs=[pl.BlockSpec((1, rows, cols), lambda i: (first + i, 0, 0))]
        + [FAR] * len(after),
        out_specs=[pl.BlockSpec((1, piece, rows), lambda i: (i, 0, 0))] * n,
        scratch_shapes=[pltpu.VMEM((cols, rows), jnp.bfloat16)],
        cost_estimate=pl.CostEstimate(
            flops=count * 4_000_000, bytes_accessed=count * rows * cols * 6, transcendentals=0
        ),
    )(x, *after)


def stats_kernel(n, piece, experts, *refs):
    gate_ref, up_ref, router_ref, gain_ref = refs[:4]
    outs = refs[-3 - n : -3]
    sums, tops, turned = refs[-3:]
    e = pl.program_id(0)
    me = lax.axis_index("shard")
    for k, ref in enumerate((gate_ref, up_ref)):
        x = ref[0]
        sums[pl.ds(k * experts + e, 1), :] = jnp.sum(x * x, axis=0, keepdims=True)
        tops[pl.ds(k * experts + e, 1), :] = column_max(x)

    @pl.when(e == experts - 1)
    def _():
        total = sums[...]
        high = total.astype(jnp.bfloat16).astype(jnp.float32)
        rest = total - high
        middle = rest.astype(jnp.bfloat16).astype(jnp.float32)
        low = rest - middle
        everything = jnp.concatenate([high, middle, low, tops[...]], axis=0)
        turned[...] = everything.T.astype(jnp.bfloat16)
        router = (router_ref[...] * gain_ref[...]).astype(jnp.bfloat16)
        half = router.shape[1] // 2
        for o in range(n):
            first = pl.multiple_of((me ^ o) * piece, 16)
            outs[o][pl.ds(0, piece), :] = turned[pl.ds(first, piece), :]
            outs[o][pl.ds(piece, experts), :] = router[:, :half]
            outs[o][pl.ds(piece + experts, experts), :] = router[:, half:]


def stats(gate, up, router, gain, n, after=()):
    experts, rows, cols = gate.shape
    piece = cols // n
    block = jax.ShapeDtypeStruct((piece + 2 * experts, 128), jnp.bfloat16)
    whole = pl.BlockSpec(memory_space=pltpu.VMEM)
    return pl.pallas_call(
        lambda *refs: stats_kernel(n, piece, experts, *refs),
        name="stats",
        grid=(experts,),
        out_shape=[block] * n,
        in_specs=[pl.BlockSpec((1, rows, cols), lambda i: (i, 0, 0))] * 2
        + [whole] * 2
        + [FAR] * len(after),
        out_specs=[whole] * n,
        scratch_shapes=[
            pltpu.VMEM((2 * experts, cols), jnp.float32),
            pltpu.VMEM((2 * experts, cols), jnp.float32),
            pltpu.VMEM((cols, 128), jnp.bfloat16),
        ],
        cost_estimate=pl.CostEstimate(
            flops=experts * 4_000_000, bytes_accessed=experts * rows * cols * 8, transcendentals=0
        ),
    )(gate, up, router, gain, *after)


def factor_kernel(n, piece, experts, rows, *refs):
    told = refs[:n]
    factor_ref, gate_ref, up_ref, router_ref = refs[n:]
    me = lax.axis_index("shard")
    w = 2 * experts
    half = rows // 2
    total, tops = None, []
    for o in range(n):
        lines = told[o][pl.ds(0, piece), :].astype(jnp.float32).T
        part = lines[:w] + lines[w : 2 * w] + lines[2 * w : 3 * w]
        total = part if total is None else total + part
        tops.append(lines[3 * w : 4 * w])
        for k in range(2):
            at = pl.multiple_of((me ^ o) * rows + k * half, half)
            router_ref[:, pl.ds(at, half)] = told[o][pl.ds(piece + k * experts, experts), :]
    scale = jnp.sqrt(total)
    gate_ref[...] = scale[:experts]
    up_ref[...] = scale[experts:]
    for o in range(n):
        factor_ref[:, o, :] = tops[o] / (SPAN * scale)


def factors(told, experts, rows, router_kind):
    n = len(told)
    piece = told[0].shape[0] - 2 * experts
    return pl.pallas_call(
        lambda *refs: factor_kernel(n, piece, experts, rows, *refs),
        name="factors",
        out_shape=[
            jax.ShapeDtypeStruct((2 * experts, n, piece), jnp.float32),
            jax.ShapeDtypeStruct((experts, piece), jnp.float32),
            jax.ShapeDtypeStruct((experts, piece), jnp.float32),
            jax.ShapeDtypeStruct((experts, n * rows), router_kind),
        ],
        cost_estimate=pl.CostEstimate(
            flops=2_000_000, bytes_accessed=3_000_000, transcendentals=0
        ),
    )(*told)


def decode_kernel(n, rows, *refs):
    factor_ref, pieces, out_ref, token_ref = refs[0], refs[1 : 1 + n], refs[-2], refs[-1]
    token_ref[...] = jnp.zeros_like(token_ref)
    me = lax.axis_index("shard")
    factor = factor_ref[0].T
    for o in range(n):
        y = pieces[o][0].astype(jnp.float32)
        v = (jnp.log2(jnp.abs(y)) + HALF) * factor[:, o : o + 1]
        v = jnp.where(y < 0, -v, v).astype(jnp.bfloat16)
        first = pl.multiple_of((me ^ o) * rows, 128)
        out_ref[0, :, pl.ds(first, rows)] = v


def decode(pieces, factor, which, first, experts, into):
    n = len(pieces)
    count, piece, rows = pieces[0].shape
    base = which * experts + first
    into = () if into is None else (into,)
    return pl.pallas_call(
        lambda *refs: decode_kernel(n, rows, *refs),
        name="decode",
        grid=(count,),
        out_shape=[
            jax.ShapeDtypeStruct((experts, piece, n * rows), jnp.bfloat16),
            jax.ShapeDtypeStruct((8, 128), jnp.float32),
        ],
        in_specs=[pl.BlockSpec((1, n, piece), lambda i: (base + i, 0, 0))]
        + [pl.BlockSpec((1, piece, rows), lambda i: (i, 0, 0))] * n
        + [FAR] * len(into),
        out_specs=[
            pl.BlockSpec((1, piece, n * rows), lambda i: (first + i, 0, 0)),
            pl.BlockSpec((8, 128), lambda i: (0, 0)),
        ],
        input_output_aliases={n + 1: 0} if into else {},
        cost_estimate=pl.CostEstimate(
            flops=count * 4_000_000, bytes_accessed=count * rows * piece * n * 4, transcendentals=0
        ),
    )(factor, *pieces, *into)


def place_kernel(axis, along, n, part, *refs):
    me = lax.axis_index(axis)
    out_ref = refs[-1]
    for o in range(n):
        first = pl.multiple_of((me ^ o) * part, part)
        at = (slice(None), pl.ds(first, part)) if along else (pl.ds(first, part), slice(None))
        out_ref[at] = refs[o][...]


def place(parts, axis, along):
    n = len(parts)
    shape = list(parts[0].shape)
    part = shape[along]
    shape[along] *= n
    return pl.pallas_call(
        lambda *refs: place_kernel(axis, along, n, part, *refs),
        name="place",
        out_shape=jax.ShapeDtypeStruct(tuple(shape), parts[0].dtype),
    )(*parts)


def swap(x, axis, n, o):
    return lax.ppermute(x, axis, [(i, i ^ o) for i in range(n)])


ORDER = (2, 4, 6, 3, 5, 7, 1)


def exchange(parts):
    n = len(parts)
    got = [parts[0]] + [None] * (n - 1)
    order = ORDER if n == 8 else range(1, n)
    for o in order:
        got[o] = swap(parts[o], "shard", n, o)
    return got


def cuts(experts):
    sizes, left = [], experts
    step = max(1, experts // 4)
    while left > 0:
        sizes.append(min(step, left))
        left -= sizes[-1]
    return sizes


def plan(experts):
    if experts == 16:
        sizes = ([2, 5, 5, 4], [5, 5, 5, 1])
    else:
        sizes = (cuts(experts), cuts(experts))
    chunks = []
    for which in range(2):
        first = 0
        for size in sizes[which]:
            chunks.append((which, first, size))
            first += size
    return chunks


AHEAD = 2


def local(groups, n, gate, up, router_weight, router_gain):
    experts, rows, _ = gate.shape
    chunks = plan(experts)
    source = (gate, up)
    result = [None, None]
    got, tokens = {}, {}

    def send(k):
        which, first, size = chunks[k]
        after = ()
        if k >= AHEAD:
            after += tuple(got[k - AHEAD][1:])
        if k - AHEAD - 1 in tokens:
            after += (tokens[k - AHEAD - 1],)
        sent = encode(source[which], first, size, n, after)
        got[k] = exchange(sent)

    def receive(k):
        which, first, _ = chunks[k]
        result[which], tokens[k] = decode(
            got[k], factor, which, first, experts, result[which]
        )

    for k in range(AHEAD):
        send(k)
    messages = stats(gate, up, router_weight.T, router_gain[None, :], n)
    messages = exchange(messages)
    factor, scale_gate, scale_up, rows_router = factors(messages, experts, rows, jnp.bfloat16)
    blocks = [rows_router] + [
        swap(rows_router, "expert", groups, o) for o in range(1, groups)
    ]
    serve_router = place(blocks, "expert", 0).T
    for k in range(AHEAD, len(chunks)):
        send(k)
        receive(k - AHEAD)
    for k in range(len(chunks) - AHEAD, len(chunks)):
        receive(k)
    return (
        result[0].transpose(0, 2, 1),
        result[1].transpose(0, 2, 1),
        scale_gate,
        scale_up,
        serve_router,
    )


def power_of_two(n):
    return n & (n - 1) == 0


def suits(groups, n, experts, rows, cols):
    return (
        power_of_two(n)
        and power_of_two(groups)
        and n <= 16
        and cols % (16 * n) == 0
        and cols % 128 == 0
        and rows == 256
        and experts == 16
    )


def solution(mesh):
    groups, n = mesh.shape["expert"], mesh.shape["shard"]

    def body(gate, up, router_weight, router_gain):
        if gate.shape == up.shape and suits(groups, n, *gate.shape):
            return local(groups, n, gate, up, router_weight, router_gain)
        return plain(gate, up, router_weight, router_gain)

    in_specs = (
        P("expert", "shard", None),
        P("expert", "shard", None),
        P("shard", "expert"),
        P("shard"),
    )
    out_specs = (
        P("expert", None, "shard"),
        P("expert", None, "shard"),
        P("expert", "shard"),
        P("expert", "shard"),
        P(),
    )
    step = jax.shard_map(body, mesh=mesh, in_specs=in_specs, out_specs=out_specs, check_vma=False)

    def whole(master_gate, master_up, router_weight, router_gain):
        experts, rows, cols = master_gate.shape
        run = step
        if suits(groups, n, experts // groups, rows // n, cols):
            run = step
        return run(master_gate, master_up, router_weight, router_gain)

    return whole
```

time: 447 us -> 355 us (0.79)
  blocking collectives: 145 us -> 0 us
  Pallas kernels: 0 us -> 118 us
  local copies, waits for them, and re-layouts: 110 us -> 5.35 us
  starting transfers between devices: 10.5 us -> 63.1 us
  other arithmetic: 44.3 us -> 0 us
  waiting for transfers between devices: 122 us -> 165 us
  between operations: 14.1 us -> 1.17 us
    ppermute x0 -> x66, waiting for transfers between devices: none -> 165 us  [swap(): return lax.ppermute(x, axis, [(i, i ^ o) for i in range(n)])]
    all_gather x2 -> x0, blocking collectives: 145 us -> none  [the longest x1 131 us: local(): row_router = lax.all_gather(part_router, 'shard', axis=0, tiled=True)]
    pallas_call x0 -> x19, Pallas kernels: none -> 118 us  [the longest x8 49.3 us: encode(): pl.pallas_call(lambda *refs: encode_kernel(n, piece, *refs), name='encode...]
    all_to_all x2 -> x0, waiting for transfers between devices: 89.5 us -> none  [the longest x1 89.5 us: local(): lax.all_to_all(narrow_up, 'shard', split_axis=2, concat_axis=1, tiled=True)]
    ppermute x0 -> x66, starting transfers between devices: none -> 63.1 us  [swap(): return lax.ppermute(x, axis, [(i, i ^ o) for i in range(n)])]
    all_to_all x4 -> x0, local copies, waits for them, and re-layouts: 58.6 us -> none  [the longest x2 29.3 us: local(): lax.all_to_all(narrow_gate, 'shard', split_axis=2, concat_axis=1, tiled=T...]
    unnamed x9 -> x128, local copies, waits for them, and re-layouts: 48.1 us -> 5.35 us
    psum x1 -> x0, waiting for transfers between devices: 32.3 us -> none  [local(): lax.psum((jnp.sum(master_gate * master_gate, axis=1), jnp.sum(master_up *...]
  transfers between devices with their start and end apart: 3 -> 66, of which waited for: 2 -> 19; matrix products, arithmetic and copies ran while one was open for 17% -> 0% of each run, Pallas kernels for 0% -> 27%
where the time goes in v1:
time: 355 us; the launch traced here: 353 us
  waiting for transfers between devices  165 us (46%)
  Pallas kernels  118 us (33%)
  starting transfers between devices  63.1 us (18%)
  local copies, waits for them, and re-layouts  5.35 us (2%)
    ppermute x66, waiting for transfers between devices, swap(): return lax.ppermute(x, axis, [(i, i ^ o) for i in range(n)])  165 us
    ppermute x66, starting transfers between devices, swap(): return lax.ppermute(x, axis, [(i, i ^ o) for i in range(n)])  63.1 us
    pallas_call x8, Pallas kernels, encode(): pl.pallas_call(lambda *refs: encode_kernel(n, piece, *refs), name='encode...  49.3 us
    pallas_call x8, Pallas kernels, decode(): pl.pallas_call(lambda *refs: decode_kernel(n, rows, *refs), name='decode'...  44.8 us
    pallas_call x1, Pallas kernels, stats(): pl.pallas_call(lambda *refs: stats_kernel(n, piece, experts, *refs), name...  20.2 us
  transfers between devices with their start and end apart: 66, of which 19 were waited for; matrix products, arithmetic and copies ran while one was open for 0% of the time, Pallas kernels for 27%

profile of v1, /device:TPU:0, one launch (start us, length us, event | category | flops | bytes accessed | tf_op | source)
XLA Modules:
  0.0 352.8 jit_solution(17121547950549649804)
XLA Ops:
  0.6 20.2 %stats.1 = (bf16[208,128]{1,0:T(8,128)(2,1)}, bf16[208,128]{1,0:T(8,128)(2,1)}, bf16[208,128]{1,0:T(8,128)(2,1)}, bf16[208,128]{1,0:T(8,128)(2,1)}, bf16[208,128...) custom-call(f32[16,256,1408]{2,1,0:T(8,128)} %refs_0_.13, ...), custom_call_target="tpu_custom_call" | custom-call | flops 64000000 | bytes 46137344 | tf_op jit(solution)/shard_map/stats/pallas_call | solution.py:107
  21.4 2.6 collective-permute-start.1
  24.1 3.4 encode.9
  27.6 2.0 collective-permute-start.3
  31.8 3.4 collective-permute-start.5
  35.2 7.4 %encode.8 = (bf16[5,176,256]{2,1,0:T(8,128)(2,1)}, bf16[5,176,256]{2,1,0:T(8,128)(2,1)}, bf16[5,176,256]{2,1,0:T(8,128)(2,1)}, bf16[5,176,256]{2,1,0:T(8,128)(2,...) custom-call(f32[16,256,1408]{2,1,0:T(8,128)} %refs_0_.13), custom_call_target="tpu_custom_call" | custom-call | flops 20000000 | bytes 10813440 | tf_op jit(solution)/shard_map/encode/pallas_call | solution.py:58
  43.6 4.2 %collective-permute-done.6.refs_7_ = bf16[208,128]{1,0:T(8,128)(2,1)S(1)} collective-permute-done((bf16[208,128]{1,0:T(8,128)(2,1)S(1)}, bf16[208,128]{1,0:T(8,128)(2,1)S(1)}, u32[]{:S(2)}, u32[]{:S(2)}) %collective-permute-start.6) | collective-permute-done | bytes 53280 | tf_op jit(solution)/shard_map/ppermute | solution.py:229
  50.4 1.7 collective-permute-start.19
  52.1 3.8 %collective-permute-done.17.refs_5_.refs_4_ = bf16[2,176,256]{2,1,0:T(8,128)(2,1)S(1)} collective-permute-done((bf16[2,176,256]{2,1,0:T(8,128)(2,1)S(1)}, bf16[2,176,256]{2,1,0:T(8,128)(2,1)S(1)}, u32[]{:S(2)}, u32[]{:S(2)}) %collective-permute-start.17) | collective-permute-done | bytes 180256 | tf_op jit(solution)/shard_map/ppermute | solution.py:229
  55.8 2.9 collective-permute-done.18.refs_6_.refs_5_
  59.1 8.1 %collective-permute-done.19.refs_7_.refs_6_ = bf16[2,176,256]{2,1,0:T(8,128)(2,1)S(1)} collective-permute-done((bf16[2,176,256]{2,1,0:T(8,128)(2,1)S(1)}, bf16[2,176,256]{2,1,0:T(8,128)(2,1)S(1)}, u32[]{:S(2)}, u32[]{:S(2)}) %collective-permute-start.19) | collective-permute-done | bytes 180256 | tf_op jit(solution)/shard_map/ppermute | solution.py:229
  73.8 7.4 %encode.11 = (bf16[5,176,256]{2,1,0:T(8,128)(2,1)}, bf16[5,176,256]{2,1,0:T(8,128)(2,1)}, bf16[5,176,256]{2,1,0:T(8,128)(2,1)}, bf16[5,176,256]{2,1,0:T(8,128)(2...) custom-call(f32[16,256,1408]{2,1,0:T(8,128)} %refs_0_.13, ...), custom_call_target="tpu_custom_call" | custom-call | flops 20000000 | bytes 10813440 | tf_op jit(solution)/shard_map/encode/pallas_call | solution.py:58
  81.8 18.8 %collective-permute-done.10.refs_4_.refs_5_ = bf16[5,176,256]{2,1,0:T(8,128)(2,1)S(1)} collective-permute-done((bf16[5,176,256]{2,1,0:T(8,128)(2,1)}, bf16[5,176,256]{2,1,0:T(8,128)(2,1)S(1)}, u32[]{:S(2)}, u32[]{:S(2)}) %collective-permute-start.10) | collective-permute-done | bytes 450592 | tf_op jit(solution)/shard_map/ppermute | solution.py:229
  100.6 6.9 %collective-permute-done.11.refs_5_.refs_6_ = bf16[5,176,256]{2,1,0:T(8,128)(2,1)S(1)} collective-permute-done((bf16[5,176,256]{2,1,0:T(8,128)(2,1)}, bf16[5,176,256]{2,1,0:T(8,128)(2,1)S(1)}, u32[]{:S(2)}, u32[]{:S(2)}) %collective-permute-start.11) | collective-permute-done | bytes 450592 | tf_op jit(solution)/shard_map/ppermute | solution.py:229
  110.5 1.8 collective-permute-start.33
  113.6 2.0 factors.1
  115.6 3.3 decode.8
  118.8 5.8 %encode.10 = (bf16[4,176,256]{2,1,0:T(8,128)(2,1)}, bf16[4,176,256]{2,1,0:T(8,128)(2,1)}, bf16[4,176,256]{2,1,0:T(8,128)(2,1)}, bf16[4,176,256]{2,1,0:T(8,128)(2...) custom-call(f32[16,256,1408]{2,1,0:T(8,128)} %refs_0_.13, ...), custom_call_target="tpu_custom_call" | custom-call | flops 16000000 | bytes 8650752 | tf_op jit(solution)/shard_map/encode/pallas_call | solution.py:58
  124.9 16.8 %collective-permute-done.31.refs_5_.refs_4_ = bf16[5,176,256]{2,1,0:T(8,128)(2,1)S(1)} collective-permute-done((bf16[5,176,256]{2,1,0:T(8,128)(2,1)}, bf16[5,176,256]{2,1,0:T(8,128)(2,1)S(1)}, u32[]{:S(2)}, u32[]{:S(2)}) %collective-permute-start.31) | collective-permute-done | bytes 450592 | tf_op jit(solution)/shard_map/ppermute | solution.py:229
  141.7 1.7 collective-permute-start.22
  143.4 6.2 %collective-permute-done.32.refs_6_.refs_5_ = bf16[5,176,256]{2,1,0:T(8,128)(2,1)S(1)} collective-permute-done((bf16[5,176,256]{2,1,0:T(8,128)(2,1)}, bf16[5,176,256]{2,1,0:T(8,128)(2,1)S(1)}, u32[]{:S(2)}, u32[]{:S(2)}) %collective-permute-start.32) | collective-permute-done | bytes 450592 | tf_op jit(solution)/shard_map/ppermute | solution.py:229
  151.8 6.7 %decode.9 = (bf16[16,176,2048]{2,1,0:T(8,128)(2,1)}, f32[8,128]{1,0:T(8,128)}) custom-call(f32[32,8,176]{2,1,0:T(8,128)} %get-tuple-element.102.refs_0_, bf16[5,176,256]{2,1,0:T(8,128)(2,1)} %get-tuple-element.135.refs_1_, bf16[5,176,256]{2,1,0:T(8,128)(2,1)} %copy-done.8, bf16[5,176,256]{2,1,0:T(8,128)(2,1)} %copy-done.12, ...), custom_call_target="tpu_custom_call", output_to_operand_aliasing={{0}: (9, {})} | custom-call | flops 20000000 | bytes 7208960 | tf_op jit(solution)/shard_map/decode/pallas_call | solution.py:185
  158.5 1.9 collective-permute-start.26
  160.4 7.5 %encode.13 = (bf16[5,176,256]{2,1,0:T(8,128)(2,1)}, bf16[5,176,256]{2,1,0:T(8,128)(2,1)}, bf16[5,176,256]{2,1,0:T(8,128)(2,1)}, bf16[5,176,256]{2,1,0:T(8,128)(2...) custom-call(f32[16,256,1408]{2,1,0:T(8,128)} %refs_0_.17, ...), custom_call_target="tpu_custom_call" | custom-call | flops 20000000 | bytes 10813440 | tf_op jit(solution)/shard_map/encode/pallas_call | solution.py:58
  171.5 11.4 %collective-permute-done.25.refs_6_.refs_5_ = bf16[4,176,256]{2,1,0:T(8,128)(2,1)} collective-permute-done((bf16[4,176,256]{2,1,0:T(8,128)(2,1)}, bf16[4,176,256]{2,1,0:T(8,128)(2,1)}, u32[]{:S(2)}, u32[]{:S(2)}) %collective-permute-start.25) | collective-permute-done | bytes 360480 | tf_op jit(solution)/shard_map/ppermute | solution.py:229
  182.9 2.4 collective-permute-start.44
  187.4 3.3 collective-permute-done.43.refs_3_.refs_2_
  191.0 6.7 %decode.10 = (bf16[16,176,2048]{2,1,0:T(8,128)(2,1)}, f32[8,128]{1,0:T(8,128)}) custom-call(f32[32,8,176]{2,1,0:T(8,128)} %get-tuple-element.102.refs_0_, bf16[5,176,256]{2,1,0:T(8,128)(2,1)} %get-tuple-element.127.refs_1_, bf16[5,176,256]{2,1,0:T(8,128)(2,1)} %copy-done.10, bf16[5,176,256]{2,1,0:T(8,128)(2,1)} %copy-done.11, ...), custom_call_target="tpu_custom_call", output_to_operand_aliasing={{0}: (9, {})} | custom-call | flops 20000000 | bytes 7208960 | tf_op jit(solution)/shard_map/decode/pallas_call | solution.py:185
  197.7 7.4 %encode.12 = (bf16[5,176,256]{2,1,0:T(8,128)(2,1)}, bf16[5,176,256]{2,1,0:T(8,128)(2,1)}, bf16[5,176,256]{2,1,0:T(8,128)(2,1)}, bf16[5,176,256]{2,1,0:T(8,128)(2...) custom-call(f32[16,256,1408]{2,1,0:T(8,128)} %refs_0_.17, ...), custom_call_target="tpu_custom_call" | custom-call | flops 20000000 | bytes 10813440 | tf_op jit(solution)/shard_map/encode/pallas_call | solution.py:58
  207.3 17.2 %collective-permute-done.46.refs_6_.refs_5_ = bf16[5,176,256]{2,1,0:T(8,128)(2,1)S(1)} collective-permute-done((bf16[5,176,256]{2,1,0:T(8,128)(2,1)}, bf16[5,176,256]{2,1,0:T(8,128)(2,1)S(1)}, u32[]{:S(2)}, u32[]{:S(2)}) %collective-permute-start.46) | collective-permute-done | bytes 450592 | tf_op jit(solution)/shard_map/ppermute | solution.py:229
  224.5 2.3 collective-permute-start.37
  227.6 1.7 collective-permute-start.40
  229.4 1.8 collective-permute-start.41
  231.2 5.3 %decode.11 = (bf16[16,176,2048]{2,1,0:T(8,128)(2,1)}, f32[8,128]{1,0:T(8,128)}) custom-call(f32[32,8,176]{2,1,0:T(8,128)} %get-tuple-element.102.refs_0_, bf16[4,176,256]{2,1,0:T(8,128)(2,1)} %get-tuple-element.119.refs_1_, bf16[4,176,256]{2,1,0:T(8,128)(2,1)} %copy-done.23, bf16[4,176,256]{2,1,0:T(8,128)(2,1)} %copy-done.24, ...), custom_call_target="tpu_custom_call", output_to_operand_aliasing={{0}: (9, {})} | custom-call | flops 16000000 | bytes 5767168 | tf_op jit(solution)/shard_map/decode/pallas_call | solution.py:185
  236.6 7.6 %encode.15 = (bf16[5,176,256]{2,1,0:T(8,128)(2,1)}, bf16[5,176,256]{2,1,0:T(8,128)(2,1)}, bf16[5,176,256]{2,1,0:T(8,128)(2,1)}, bf16[5,176,256]{2,1,0:T(8,128)(2...) custom-call(f32[16,256,1408]{2,1,0:T(8,128)} %refs_0_.17, ...), custom_call_target="tpu_custom_call" | custom-call | flops 20000000 | bytes 10813440 | tf_op jit(solution)/shard_map/encode/pallas_call | solution.py:58
  244.3 15.3 %collective-permute-done.38.refs_4_.refs_5_ = bf16[5,176,256]{2,1,0:T(8,128)(2,1)} collective-permute-done((bf16[5,176,256]{2,1,0:T(8,128)(2,1)}, bf16[5,176,256]{2,1,0:T(8,128)(2,1)}, u32[]{:S(2)}, u32[]{:S(2)}) %collective-permute-start.38) | collective-permute-done | bytes 450592 | tf_op jit(solution)/shard_map/ppermute | solution.py:229
  260.7 5.6 %collective-permute-done.39.refs_5_.refs_6_ = bf16[5,176,256]{2,1,0:T(8,128)(2,1)} collective-permute-done((bf16[5,176,256]{2,1,0:T(8,128)(2,1)}, bf16[5,176,256]{2,1,0:T(8,128)(2,1)}, u32[]{:S(2)}, u32[]{:S(2)}) %collective-permute-start.39) | collective-permute-done | bytes 450592 | tf_op jit(solution)/shard_map/ppermute | solution.py:229
  267.0 2.6 collective-permute-start.64
  269.6 6.7 %decode.12 = (bf16[16,176,2048]{2,1,0:T(8,128)(2,1)}, f32[8,128]{1,0:T(8,128)}) custom-call(f32[32,8,176]{2,1,0:T(8,128)} %get-tuple-element.102.refs_0_, bf16[5,176,256]{2,1,0:T(8,128)(2,1)} %get-tuple-element.149.refs_1_, bf16[5,176,256]{2,1,0:T(8,128)(2,1)} %copy-done, bf16[5,176,256]{2,1,0:T(8,128)(2,1)} %copy-done.1, bf16[5,176,256]{2,1,0:T(8,128)(2,1)} %copy-done.2, ...), custom_call_target="tpu_custom_call" | custom-call | flops 20000000 | bytes 7208960 | tf_op jit(solution)/shard_map/decode/pallas_call | solution.py:185
  276.3 2.8 encode.14
  282.8 5.2 %collective-permute-done.65.refs_3_ = bf16[16,2048]{1,0:T(8,128)(2,1)S(1)} collective-permute-done((bf16[16,2048]{1,0:T(8,128)(2,1)S(1)}, bf16[16,2048]{1,0:T(8,128)(2,1)S(1)}, u32[]{:S(2)}, u32[]{:S(2)}) %collective-permute-start.65) | collective-permute-done | bytes 65568 | tf_op jit(solution)/shard_map/ppermute | solution.py:229
  293.1 8.4 %collective-permute-done.58.refs_4_ = bf16[5,176,256]{2,1,0:T(8,128)(2,1)S(1)} collective-permute-done((bf16[5,176,256]{2,1,0:T(8,128)(2,1)}, bf16[5,176,256]{2,1,0:T(8,128)(2,1)S(1)}, u32[]{:S(2)}, u32[]{:S(2)}) %collective-permute-start.58) | collective-permute-done | bytes 450592 | tf_op jit(solution)/shard_map/ppermute | solution.py:229
  301.5 19.9 %collective-permute-done.59.refs_5_ = bf16[5,176,256]{2,1,0:T(8,128)(2,1)S(1)} collective-permute-done((bf16[5,176,256]{2,1,0:T(8,128)(2,1)}, bf16[5,176,256]{2,1,0:T(8,128)(2,1)S(1)}, u32[]{:S(2)}, u32[]{:S(2)}) %collective-permute-start.59) | collective-permute-done | bytes 450592 | tf_op jit(solution)/shard_map/ppermute | solution.py:229
  321.7 9.1 %collective-permute-done.60.refs_6_ = bf16[5,176,256]{2,1,0:T(8,128)(2,1)S(1)} collective-permute-done((bf16[5,176,256]{2,1,0:T(8,128)(2,1)}, bf16[5,176,256]{2,1,0:T(8,128)(2,1)S(1)}, u32[]{:S(2)}, u32[]{:S(2)}) %collective-permute-start.60) | collective-permute-done | bytes 450592 | tf_op jit(solution)/shard_map/ppermute | solution.py:229
  334.2 1.7 place.1
  335.9 6.7 %decode.13 = (bf16[16,176,2048]{2,1,0:T(8,128)(2,1)}, f32[8,128]{1,0:T(8,128)}) custom-call(f32[32,8,176]{2,1,0:T(8,128)} %get-tuple-element.102.refs_0_, bf16[5,176,256]{2,1,0:T(8,128)(2,1)} %get-tuple-element.175.refs_1_, bf16[5,176,256]{2,1,0:T(8,128)(2,1)} %copy-done.7, bf16[5,176,256]{2,1,0:T(8,128)(2,1)} %copy-done.9, ...), custom_call_target="tpu_custom_call", output_to_operand_aliasing={{0}: (9, {})} | custom-call | flops 20000000 | bytes 7208960 | tf_op jit(solution)/shard_map/decode/pallas_call | solution.py:185
  342.7 6.7 %decode.14 = (bf16[16,176,2048]{2,1,0:T(8,128)(2,1)}, f32[8,128]{1,0:T(8,128)}) custom-call(f32[32,8,176]{2,1,0:T(8,128)} %get-tuple-element.102.refs_0_, bf16[5,176,256]{2,1,0:T(8,128)(2,1)} %get-tuple-element.167.refs_1_, bf16[5,176,256]{2,1,0:T(8,128)(2,1)} %copy-done.34, bf16[5,176,256]{2,1,0:T(8,128)(2,1)} %copy-done.35, ...), custom_call_target="tpu_custom_call", output_to_operand_aliasing={{0}: (9, {})} | custom-call | flops 20000000 | bytes 7208960 | tf_op jit(solution)/shard_map/decode/pallas_call | solution.py:185
  350.1 2.6 decode.15
  (231 shorter events, 44.5 us)
Async XLA Ops:
  27.5 21.0 %collective-permute-start.14 = (bf16[2,176,256]{2,1,0:T(8,128)(2,1)}, bf16[2,176,256]{2,1,0:T(8,128)(2,1)S(1)}, u32[]{:S(2)}, u32[]{:S(2)}) collective-permute-start(bf16[2,176,256]{2,1,0:T(8,128)(2,1)} %get-tuple-element.111), channel_id=1, source_target_pairs={{0,1},{1,0},{2,3},{3,2},{4,5},{5,4},{6,7},{7,6},{8,9},{9,8},{10,11... | collective-permute-start | bytes 540680 | tf_op jit(solution)/shard_map/ppermute | solution.py:229
  29.6 19.9 %collective-permute-start.15 = (bf16[2,176,256]{2,1,0:T(8,128)(2,1)}, bf16[2,176,256]{2,1,0:T(8,128)(2,1)S(1)}, u32[]{:S(2)}, u32[]{:S(2)}) collective-permute-start(bf16[2,176,256]{2,1,0:T(8,128)(2,1)} %get-tuple-element.112), channel_id=1, source_target_pairs={{0,2},{1,3},{2,0},{3,1},{4,6},{5,7},{6,4},{7,5},{8,10},{9,11},{10,... | collective-permute-start | bytes 540680 | tf_op jit(solution)/shard_map/ppermute | solution.py:229
  31.2 19.2 %collective-permute-start.16 = (bf16[2,176,256]{2,1,0:T(8,128)(2,1)}, bf16[2,176,256]{2,1,0:T(8,128)(2,1)S(1)}, u32[]{:S(2)}, u32[]{:S(2)}) collective-permute-start(bf16[2,176,256]{2,1,0:T(8,128)(2,1)} %get-tuple-element.113), channel_id=1, source_target_pairs={{0,3},{1,2},{2,1},{3,0},{4,7},{5,6},{6,5},{7,4},{8,11},{9,10},{10,... | collective-permute-start | bytes 540680 | tf_op jit(solution)/shard_map/ppermute | solution.py:229
  43.2 28.0 %collective-permute-start.7 = (bf16[5,176,256]{2,1,0:T(8,128)(2,1)}, bf16[5,176,256]{2,1,0:T(8,128)(2,1)S(1)}, u32[]{:S(2)}, u32[]{:S(2)}) collective-permute-start(bf16[5,176,256]{2,1,0:T(8,128)(2,1)} %get-tuple-element.103), channel_id=1, source_target_pairs={{0,1},{1,0},{2,3},{3,2},{4,5},{5,4},{6,7},{7,6},{8,9},{9,8},{10,11... | collective-permute-start | bytes 1351688 | tf_op jit(solution)/shard_map/ppermute | solution.py:229
  48.4 24.2 %collective-permute-start.8 = (bf16[5,176,256]{2,1,0:T(8,128)(2,1)}, bf16[5,176,256]{2,1,0:T(8,128)(2,1)S(1)}, u32[]{:S(2)}, u32[]{:S(2)}) collective-permute-start(bf16[5,176,256]{2,1,0:T(8,128)(2,1)} %get-tuple-element.104), channel_id=1, source_target_pairs={{0,2},{1,3},{2,0},{3,1},{4,6},{5,7},{6,4},{7,5},{8,10},{9,11},{10,... | collective-permute-start | bytes 1351688 | tf_op jit(solution)/shard_map/ppermute | solution.py:229
  50.4 16.8 %collective-permute-start.19 = (bf16[2,176,256]{2,1,0:T(8,128)(2,1)S(1)}, bf16[2,176,256]{2,1,0:T(8,128)(2,1)S(1)}, u32[]{:S(2)}, u32[]{:S(2)}) collective-permute-start(bf16[2,176,256]{2,1,0:T(8,128)(2,1)S(1)} %copy-done.57), channel_id=1, source_target_pairs={{0,6},{1,7},{2,4},{3,5},{4,2},{5,3},{6,0},{7,1},{8,14},{9,15},{10,... | collective-permute-start | bytes 540680 | tf_op jit(solution)/shard_map/ppermute | solution.py:229
  58.7 22.5 %collective-permute-start.9 = (bf16[5,176,256]{2,1,0:T(8,128)(2,1)}, bf16[5,176,256]{2,1,0:T(8,128)(2,1)S(1)}, u32[]{:S(2)}, u32[]{:S(2)}) collective-permute-start(bf16[5,176,256]{2,1,0:T(8,128)(2,1)} %get-tuple-element.105), channel_id=1, source_target_pairs={{0,3},{1,2},{2,1},{3,0},{4,7},{5,6},{6,5},{7,4},{8,11},{9,10},{10,... | collective-permute-start | bytes 1351688 | tf_op jit(solution)/shard_map/ppermute | solution.py:229
  67.8 32.7 %collective-permute-start.10 = (bf16[5,176,256]{2,1,0:T(8,128)(2,1)}, bf16[5,176,256]{2,1,0:T(8,128)(2,1)S(1)}, u32[]{:S(2)}, u32[]{:S(2)}) collective-permute-start(bf16[5,176,256]{2,1,0:T(8,128)(2,1)} %get-tuple-element.106), channel_id=1, source_target_pairs={{0,4},{1,5},{2,6},{3,7},{4,0},{5,1},{6,2},{7,3},{8,12},{9,13},{10,... | collective-permute-start | bytes 1351688 | tf_op jit(solution)/shard_map/ppermute | solution.py:229
  70.2 37.3 %collective-permute-start.11 = (bf16[5,176,256]{2,1,0:T(8,128)(2,1)}, bf16[5,176,256]{2,1,0:T(8,128)(2,1)S(1)}, u32[]{:S(2)}, u32[]{:S(2)}) collective-permute-start(bf16[5,176,256]{2,1,0:T(8,128)(2,1)} %get-tuple-element.107), channel_id=1, source_target_pairs={{0,5},{1,4},{2,7},{3,6},{4,1},{5,0},{6,3},{7,2},{8,13},{9,12},{10,... | collective-permute-start | bytes 1351688 | tf_op jit(solution)/shard_map/ppermute | solution.py:229
  71.2 37.7 %collective-permute-start.12 = (bf16[5,176,256]{2,1,0:T(8,128)(2,1)}, bf16[5,176,256]{2,1,0:T(8,128)(2,1)S(1)}, u32[]{:S(2)}, u32[]{:S(2)}) collective-permute-start(bf16[5,176,256]{2,1,0:T(8,128)(2,1)} %get-tuple-element.108), channel_id=1, source_target_pairs={{0,6},{1,7},{2,4},{3,5},{4,2},{5,3},{6,0},{7,1},{8,14},{9,15},{10,... | collective-permute-start | bytes 1351688 | tf_op jit(solution)/shard_map/ppermute | solution.py:229
  72.7 36.9 %collective-permute-start.13 = (bf16[5,176,256]{2,1,0:T(8,128)(2,1)}, bf16[5,176,256]{2,1,0:T(8,128)(2,1)S(1)}, u32[]{:S(2)}, u32[]{:S(2)}) collective-permute-start(bf16[5,176,256]{2,1,0:T(8,128)(2,1)} %get-tuple-element.109), channel_id=1, source_target_pairs={{0,7},{1,6},{2,5},{3,4},{4,3},{5,2},{6,1},{7,0},{8,15},{9,14},{10,... | collective-permute-start | bytes 1351688 | tf_op jit(solution)/shard_map/ppermute | solution.py:229
  81.3 29.2 %collective-permute-start.28 = (bf16[5,176,256]{2,1,0:T(8,128)(2,1)}, bf16[5,176,256]{2,1,0:T(8,128)(2,1)S(1)}, u32[]{:S(2)}, u32[]{:S(2)}) collective-permute-start(bf16[5,176,256]{2,1,0:T(8,128)(2,1)} %get-tuple-element.128), channel_id=1, source_target_pairs={{0,1},{1,0},{2,3},{3,2},{4,5},{5,4},{6,7},{7,6},{8,9},{9,8},{10,11... | collective-permute-start | bytes 1351688 | tf_op jit(solution)/shard_map/ppermute | solution.py:229
  107.5 17.1 %collective-permute-start.30 = (bf16[5,176,256]{2,1,0:T(8,128)(2,1)}, bf16[5,176,256]{2,1,0:T(8,128)(2,1)S(1)}, u32[]{:S(2)}, u32[]{:S(2)}) collective-permute-start(bf16[5,176,256]{2,1,0:T(8,128)(2,1)} %get-tuple-element.130), channel_id=1, source_target_pairs={{0,3},{1,2},{2,1},{3,0},{4,7},{5,6},{6,5},{7,4},{8,11},{9,10},{10,... | collective-permute-start | bytes 1351688 | tf_op jit(solution)/shard_map/ppermute | solution.py:229
  108.9 32.8 %collective-permute-start.31 = (bf16[5,176,256]{2,1,0:T(8,128)(2,1)}, bf16[5,176,256]{2,1,0:T(8,128)(2,1)S(1)}, u32[]{:S(2)}, u32[]{:S(2)}) collective-permute-start(bf16[5,176,256]{2,1,0:T(8,128)(2,1)} %get-tuple-element.131), channel_id=1, source_target_pairs={{0,4},{1,5},{2,6},{3,7},{4,0},{5,1},{6,2},{7,3},{8,12},{9,13},{10,... | collective-permute-start | bytes 1351688 | tf_op jit(solution)/shard_map/ppermute | solution.py:229
  109.5 40.2 %collective-permute-start.32 = (bf16[5,176,256]{2,1,0:T(8,128)(2,1)}, bf16[5,176,256]{2,1,0:T(8,128)(2,1)S(1)}, u32[]{:S(2)}, u32[]{:S(2)}) collective-permute-start(bf16[5,176,256]{2,1,0:T(8,128)(2,1)} %get-tuple-element.132), channel_id=1, source_target_pairs={{0,5},{1,4},{2,7},{3,6},{4,1},{5,0},{6,3},{7,2},{8,13},{9,12},{10,... | collective-permute-start | bytes 1351688 | tf_op jit(solution)/shard_map/ppermute | solution.py:229
  110.5 40.3 %collective-permute-start.33 = (bf16[5,176,256]{2,1,0:T(8,128)(2,1)}, bf16[5,176,256]{2,1,0:T(8,128)(2,1)S(1)}, u32[]{:S(2)}, u32[]{:S(2)}) collective-permute-start(bf16[5,176,256]{2,1,0:T(8,128)(2,1)} %get-tuple-element.133), channel_id=1, source_target_pairs={{0,6},{1,7},{2,4},{3,5},{4,2},{5,3},{6,0},{7,1},{8,14},{9,15},{10,... | collective-permute-start | bytes 1351688 | tf_op jit(solution)/shard_map/ppermute | solution.py:229
  112.4 39.3 %collective-permute-start.34 = (bf16[5,176,256]{2,1,0:T(8,128)(2,1)}, bf16[5,176,256]{2,1,0:T(8,128)(2,1)S(1)}, u32[]{:S(2)}, u32[]{:S(2)}) collective-permute-start(bf16[5,176,256]{2,1,0:T(8,128)(2,1)} %get-tuple-element.134), channel_id=1, source_target_pairs={{0,7},{1,6},{2,5},{3,4},{4,3},{5,2},{6,1},{7,0},{8,15},{9,14},{10,... | collective-permute-start | bytes 1351688 | tf_op jit(solution)/shard_map/ppermute | solution.py:229
  124.7 33.8 %collective-permute-start.21 = (bf16[4,176,256]{2,1,0:T(8,128)(2,1)}, bf16[4,176,256]{2,1,0:T(8,128)(2,1)S(1)}, u32[]{:S(2)}, u32[]{:S(2)}) collective-permute-start(bf16[4,176,256]{2,1,0:T(8,128)(2,1)} %get-tuple-element.120), channel_id=1, source_target_pairs={{0,1},{1,0},{2,3},{3,2},{4,5},{5,4},{6,7},{7,6},{8,9},{9,8},{10,11... | collective-permute-start | bytes 1081352 | tf_op jit(solution)/shard_map/ppermute | solution.py:229
  141.7 26.2 %collective-permute-start.22 = (bf16[4,176,256]{2,1,0:T(8,128)(2,1)}, bf16[4,176,256]{2,1,0:T(8,128)(2,1)S(1)}, u32[]{:S(2)}, u32[]{:S(2)}) collective-permute-start(bf16[4,176,256]{2,1,0:T(8,128)(2,1)} %get-tuple-element.121), channel_id=1, source_target_pairs={{0,2},{1,3},{2,0},{3,1},{4,6},{5,7},{6,4},{7,5},{8,10},{9,11},{10,... | collective-permute-start | bytes 1081352 | tf_op jit(solution)/shard_map/ppermute | solution.py:229
  149.7 19.0 %collective-permute-start.23 = (bf16[4,176,256]{2,1,0:T(8,128)(2,1)}, bf16[4,176,256]{2,1,0:T(8,128)(2,1)S(1)}, u32[]{:S(2)}, u32[]{:S(2)}) collective-permute-start(bf16[4,176,256]{2,1,0:T(8,128)(2,1)} %get-tuple-element.122), channel_id=1, source_target_pairs={{0,3},{1,2},{2,1},{3,0},{4,7},{5,6},{6,5},{7,4},{8,11},{9,10},{10,... | collective-permute-start | bytes 1081352 | tf_op jit(solution)/shard_map/ppermute | solution.py:229
  150.8 19.5 %collective-permute-start.24 = (bf16[4,176,256]{2,1,0:T(8,128)(2,1)}, bf16[4,176,256]{2,1,0:T(8,128)(2,1)}, u32[]{:S(2)}, u32[]{:S(2)}) collective-permute-start(bf16[4,176,256]{2,1,0:T(8,128)(2,1)} %get-tuple-element.123), channel_id=1, source_target_pairs={{0,4},{1,5},{2,6},{3,7},{4,0},{5,1},{6,2},{7,3},{8,12},{9,13},{10,... | collective-permute-start | bytes 1081352 | tf_op jit(solution)/shard_map/ppermute | solution.py:229
  151.6 31.3 %collective-permute-start.25 = (bf16[4,176,256]{2,1,0:T(8,128)(2,1)}, bf16[4,176,256]{2,1,0:T(8,128)(2,1)}, u32[]{:S(2)}, u32[]{:S(2)}) collective-permute-start(bf16[4,176,256]{2,1,0:T(8,128)(2,1)} %get-tuple-element.124), channel_id=1, source_target_pairs={{0,5},{1,4},{2,7},{3,6},{4,1},{5,0},{6,3},{7,2},{8,13},{9,12},{10,... | collective-permute-start | bytes 1081352 | tf_op jit(solution)/shard_map/ppermute | solution.py:229
  158.5 26.7 %collective-permute-start.26 = (bf16[4,176,256]{2,1,0:T(8,128)(2,1)}, bf16[4,176,256]{2,1,0:T(8,128)(2,1)}, u32[]{:S(2)}, u32[]{:S(2)}) collective-permute-start(bf16[4,176,256]{2,1,0:T(8,128)(2,1)} %get-tuple-element.125), channel_id=1, source_target_pairs={{0,6},{1,7},{2,4},{3,5},{4,2},{5,3},{6,0},{7,1},{8,14},{9,15},{10,... | collective-permute-start | bytes 1081352 | tf_op jit(solution)/shard_map/ppermute | solution.py:229
  168.7 17.3 %collective-permute-start.42 = (bf16[5,176,256]{2,1,0:T(8,128)(2,1)}, bf16[5,176,256]{2,1,0:T(8,128)(2,1)S(1)}, u32[]{:S(2)}, u32[]{:S(2)}) collective-permute-start(bf16[5,176,256]{2,1,0:T(8,128)(2,1)} %get-tuple-element.150), channel_id=1, source_target_pairs={{0,1},{1,0},{2,3},{3,2},{4,5},{5,4},{6,7},{7,6},{8,9},{9,8},{10,11... | collective-permute-start | bytes 1351688 | tf_op jit(solution)/shard_map/ppermute | solution.py:229
  168.7 17.0 %collective-permute-start.27 = (bf16[4,176,256]{2,1,0:T(8,128)(2,1)}, bf16[4,176,256]{2,1,0:T(8,128)(2,1)S(1)}, u32[]{:S(2)}, u32[]{:S(2)}) collective-permute-start(bf16[4,176,256]{2,1,0:T(8,128)(2,1)} %get-tuple-element.126), channel_id=1, source_target_pairs={{0,7},{1,6},{2,5},{3,4},{4,3},{5,2},{6,1},{7,0},{8,15},{9,14},{10,... | collective-permute-start | bytes 1081352 | tf_op jit(solution)/shard_map/ppermute | solution.py:229
  170.4 20.3 %collective-permute-start.43 = (bf16[5,176,256]{2,1,0:T(8,128)(2,1)}, bf16[5,176,256]{2,1,0:T(8,128)(2,1)S(1)}, u32[]{:S(2)}, u32[]{:S(2)}) collective-permute-start(bf16[5,176,256]{2,1,0:T(8,128)(2,1)} %get-tuple-element.151), channel_id=1, source_target_pairs={{0,2},{1,3},{2,0},{3,1},{4,6},{5,7},{6,4},{7,5},{8,10},{9,11},{10,... | collective-permute-start | bytes 1351688 | tf_op jit(solution)/shard_map/ppermute | solution.py:229
  182.9 22.3 %collective-permute-start.44 = (bf16[5,176,256]{2,1,0:T(8,128)(2,1)}, bf16[5,176,256]{2,1,0:T(8,128)(2,1)S(1)}, u32[]{:S(2)}, u32[]{:S(2)}) collective-permute-start(bf16[5,176,256]{2,1,0:T(8,128)(2,1)} %get-tuple-element.152), channel_id=1, source_target_pairs={{0,3},{1,2},{2,1},{3,0},{4,7},{5,6},{6,5},{7,4},{8,11},{9,10},{10,... | collective-permute-start | bytes 1351688 | tf_op jit(solution)/shard_map/ppermute | solution.py:229
  185.3 20.9 %collective-permute-start.45 = (bf16[5,176,256]{2,1,0:T(8,128)(2,1)}, bf16[5,176,256]{2,1,0:T(8,128)(2,1)S(1)}, u32[]{:S(2)}, u32[]{:S(2)}) collective-permute-start(bf16[5,176,256]{2,1,0:T(8,128)(2,1)} %get-tuple-element.153), channel_id=1, source_target_pairs={{0,4},{1,5},{2,6},{3,7},{4,0},{5,1},{6,2},{7,3},{8,12},{9,13},{10,... | collective-permute-start | bytes 1351688 | tf_op jit(solution)/shard_map/ppermute | solution.py:229
  185.8 38.7 %collective-permute-start.46 = (bf16[5,176,256]{2,1,0:T(8,128)(2,1)}, bf16[5,176,256]{2,1,0:T(8,128)(2,1)S(1)}, u32[]{:S(2)}, u32[]{:S(2)}) collective-permute-start(bf16[5,176,256]{2,1,0:T(8,128)(2,1)} %get-tuple-element.154), channel_id=1, source_target_pairs={{0,5},{1,4},{2,7},{3,6},{4,1},{5,0},{6,3},{7,2},{8,13},{9,12},{10,... | collective-permute-start | bytes 1351688 | tf_op jit(solution)/shard_map/ppermute | solution.py:229
  186.0 40.8 %collective-permute-start.47 = (bf16[5,176,256]{2,1,0:T(8,128)(2,1)}, bf16[5,176,256]{2,1,0:T(8,128)(2,1)S(1)}, u32[]{:S(2)}, u32[]{:S(2)}) collective-permute-start(bf16[5,176,256]{2,1,0:T(8,128)(2,1)} %get-tuple-element.155), channel_id=1, source_target_pairs={{0,6},{1,7},{2,4},{3,5},{4,2},{5,3},{6,0},{7,1},{8,14},{9,15},{10,... | collective-permute-start | bytes 1351688 | tf_op jit(solution)/shard_map/ppermute | solution.py:229
  190.7 36.6 %collective-permute-start.48 = (bf16[5,176,256]{2,1,0:T(8,128)(2,1)}, bf16[5,176,256]{2,1,0:T(8,128)(2,1)S(1)}, u32[]{:S(2)}, u32[]{:S(2)}) collective-permute-start(bf16[5,176,256]{2,1,0:T(8,128)(2,1)} %get-tuple-element.156), channel_id=1, source_target_pairs={{0,7},{1,6},{2,5},{3,4},{4,3},{5,2},{6,1},{7,0},{8,15},{9,14},{10,... | collective-permute-start | bytes 1351688 | tf_op jit(solution)/shard_map/ppermute | solution.py:229
  205.2 22.5 %collective-permute-start.35 = (bf16[5,176,256]{2,1,0:T(8,128)(2,1)}, bf16[5,176,256]{2,1,0:T(8,128)(2,1)S(1)}, u32[]{:S(2)}, u32[]{:S(2)}) collective-permute-start(bf16[5,176,256]{2,1,0:T(8,128)(2,1)} %get-tuple-element.141), channel_id=1, source_target_pairs={{0,1},{1,0},{2,3},{3,2},{4,5},{5,4},{6,7},{7,6},{8,9},{9,8},{10,11... | collective-permute-start | bytes 1351688 | tf_op jit(solution)/shard_map/ppermute | solution.py:229
  206.1 23.3 %collective-permute-start.36 = (bf16[5,176,256]{2,1,0:T(8,128)(2,1)}, bf16[5,176,256]{2,1,0:T(8,128)(2,1)S(1)}, u32[]{:S(2)}, u32[]{:S(2)}) collective-permute-start(bf16[5,176,256]{2,1,0:T(8,128)(2,1)} %get-tuple-element.142), channel_id=1, source_target_pairs={{0,2},{1,3},{2,0},{3,1},{4,6},{5,7},{6,4},{7,5},{8,10},{9,11},{10,... | collective-permute-start | bytes 1351688 | tf_op jit(solution)/shard_map/ppermute | solution.py:229
  224.5 19.7 %collective-permute-start.37 = (bf16[5,176,256]{2,1,0:T(8,128)(2,1)}, bf16[5,176,256]{2,1,0:T(8,128)(2,1)}, u32[]{:S(2)}, u32[]{:S(2)}) collective-permute-start(bf16[5,176,256]{2,1,0:T(8,128)(2,1)} %get-tuple-element.143), channel_id=1, source_target_pairs={{0,3},{1,2},{2,1},{3,0},{4,7},{5,6},{6,5},{7,4},{8,11},{9,10},{10,... | collective-permute-start | bytes 1351688 | tf_op jit(solution)/shard_map/ppermute | solution.py:229
  226.8 32.8 %collective-permute-start.38 = (bf16[5,176,256]{2,1,0:T(8,128)(2,1)}, bf16[5,176,256]{2,1,0:T(8,128)(2,1)}, u32[]{:S(2)}, u32[]{:S(2)}) collective-permute-start(bf16[5,176,256]{2,1,0:T(8,128)(2,1)} %get-tuple-element.144), channel_id=1, source_target_pairs={{0,4},{1,5},{2,6},{3,7},{4,0},{5,1},{6,2},{7,3},{8,12},{9,13},{10,... | collective-permute-start | bytes 1351688 | tf_op jit(solution)/shard_map/ppermute | solution.py:229
  227.3 39.0 %collective-permute-start.39 = (bf16[5,176,256]{2,1,0:T(8,128)(2,1)}, bf16[5,176,256]{2,1,0:T(8,128)(2,1)}, u32[]{:S(2)}, u32[]{:S(2)}) collective-permute-start(bf16[5,176,256]{2,1,0:T(8,128)(2,1)} %get-tuple-element.145), channel_id=1, source_target_pairs={{0,5},{1,4},{2,7},{3,6},{4,1},{5,0},{6,3},{7,2},{8,13},{9,12},{10,... | collective-permute-start | bytes 1351688 | tf_op jit(solution)/shard_map/ppermute | solution.py:229
  227.6 39.3 %collective-permute-start.40 = (bf16[5,176,256]{2,1,0:T(8,128)(2,1)}, bf16[5,176,256]{2,1,0:T(8,128)(2,1)}, u32[]{:S(2)}, u32[]{:S(2)}) collective-permute-start(bf16[5,176,256]{2,1,0:T(8,128)(2,1)} %get-tuple-element.146), channel_id=1, source_target_pairs={{0,6},{1,7},{2,4},{3,5},{4,2},{5,3},{6,0},{7,1},{8,14},{9,15},{10,... | collective-permute-start | bytes 1351688 | tf_op jit(solution)/shard_map/ppermute | solution.py:229
  229.4 46.9 %collective-permute-start.41 = (bf16[5,176,256]{2,1,0:T(8,128)(2,1)}, bf16[5,176,256]{2,1,0:T(8,128)(2,1)}, u32[]{:S(2)}, u32[]{:S(2)}) collective-permute-start(bf16[5,176,256]{2,1,0:T(8,128)(2,1)} %get-tuple-element.147), channel_id=1, source_target_pairs={{0,7},{1,6},{2,5},{3,4},{4,3},{5,2},{6,1},{7,0},{8,15},{9,14},{10,... | collective-permute-start | bytes 1351688 | tf_op jit(solution)/shard_map/ppermute | solution.py:229
  244.2 46.7 %collective-permute-start.56 = (bf16[5,176,256]{2,1,0:T(8,128)(2,1)}, bf16[5,176,256]{2,1,0:T(8,128)(2,1)S(1)}, u32[]{:S(2)}, u32[]{:S(2)}) collective-permute-start(bf16[5,176,256]{2,1,0:T(8,128)(2,1)} %get-tuple-element.168), channel_id=1, source_target_pairs={{0,1},{1,0},{2,3},{3,2},{4,5},{5,4},{6,7},{7,6},{8,9},{9,8},{10,11... | collective-permute-start | bytes 1351688 | tf_op jit(solution)/shard_map/ppermute | solution.py:229
  259.7 32.6 %collective-permute-start.57 = (bf16[5,176,256]{2,1,0:T(8,128)(2,1)}, bf16[5,176,256]{2,1,0:T(8,128)(2,1)S(1)}, u32[]{:S(2)}, u32[]{:S(2)}) collective-permute-start(bf16[5,176,256]{2,1,0:T(8,128)(2,1)} %get-tuple-element.169), channel_id=1, source_target_pairs={{0,2},{1,3},{2,0},{3,1},{4,6},{5,7},{6,4},{7,5},{8,10},{9,11},{10,... | collective-permute-start | bytes 1351688 | tf_op jit(solution)/shard_map/ppermute | solution.py:229
  288.6 32.8 %collective-permute-start.59 = (bf16[5,176,256]{2,1,0:T(8,128)(2,1)}, bf16[5,176,256]{2,1,0:T(8,128)(2,1)S(1)}, u32[]{:S(2)}, u32[]{:S(2)}) collective-permute-start(bf16[5,176,256]{2,1,0:T(8,128)(2,1)} %get-tuple-element.171), channel_id=1, source_target_pairs={{0,4},{1,5},{2,6},{3,7},{4,0},{5,1},{6,2},{7,3},{8,12},{9,13},{10,... | collective-permute-start | bytes 1351688 | tf_op jit(solution)/shard_map/ppermute | solution.py:229
  289.4 41.5 %collective-permute-start.60 = (bf16[5,176,256]{2,1,0:T(8,128)(2,1)}, bf16[5,176,256]{2,1,0:T(8,128)(2,1)S(1)}, u32[]{:S(2)}, u32[]{:S(2)}) collective-permute-start(bf16[5,176,256]{2,1,0:T(8,128)(2,1)} %get-tuple-element.172), channel_id=1, source_target_pairs={{0,5},{1,4},{2,7},{3,6},{4,1},{5,0},{6,3},{7,2},{8,13},{9,12},{10,... | collective-permute-start | bytes 1351688 | tf_op jit(solution)/shard_map/ppermute | solution.py:229
  290.9 40.5 %collective-permute-start.61 = (bf16[5,176,256]{2,1,0:T(8,128)(2,1)}, bf16[5,176,256]{2,1,0:T(8,128)(2,1)S(1)}, u32[]{:S(2)}, u32[]{:S(2)}) collective-permute-start(bf16[5,176,256]{2,1,0:T(8,128)(2,1)} %get-tuple-element.173), channel_id=1, source_target_pairs={{0,6},{1,7},{2,4},{3,5},{4,2},{5,3},{6,0},{7,1},{8,14},{9,15},{10,... | collective-permute-start | bytes 1351688 | tf_op jit(solution)/shard_map/ppermute | solution.py:229
  292.2 40.6 %collective-permute-start.62 = (bf16[5,176,256]{2,1,0:T(8,128)(2,1)}, bf16[5,176,256]{2,1,0:T(8,128)(2,1)S(1)}, u32[]{:S(2)}, u32[]{:S(2)}) collective-permute-start(bf16[5,176,256]{2,1,0:T(8,128)(2,1)} %get-tuple-element.174), channel_id=1, source_target_pairs={{0,7},{1,6},{2,5},{3,4},{4,3},{5,2},{6,1},{7,0},{8,15},{9,14},{10,... | collective-permute-start | bytes 1351688 | tf_op jit(solution)/shard_map/ppermute | solution.py:229
  301.4 48.0 %collective-permute-start.51 = (bf16[1,176,256]{2,1,0:T(8,128)(2,1)}, bf16[1,176,256]{2,1,0:T(8,128)(2,1)S(1)}, u32[]{:S(2)}, u32[]{:S(2)}) collective-permute-start(bf16[1,176,256]{2,1,0:T(8,128)(2,1)} %get-tuple-element.161), channel_id=1, source_target_pairs={{0,3},{1,2},{2,1},{3,0},{4,7},{5,6},{6,5},{7,4},{8,11},{9,10},{10,... | collective-permute-start | bytes 270344 | tf_op jit(solution)/shard_map/ppermute | solution.py:229
  321.4 28.1 %collective-permute-start.52 = (bf16[1,176,256]{2,1,0:T(8,128)(2,1)}, bf16[1,176,256]{2,1,0:T(8,128)(2,1)S(1)}, u32[]{:S(2)}, u32[]{:S(2)}) collective-permute-start(bf16[1,176,256]{2,1,0:T(8,128)(2,1)} %get-tuple-element.162), channel_id=1, source_target_pairs={{0,4},{1,5},{2,6},{3,7},{4,0},{5,1},{6,2},{7,3},{8,12},{9,13},{10,... | collective-permute-start | bytes 270344 | tf_op jit(solution)/shard_map/ppermute | solution.py:229
  330.9 18.6 %collective-permute-start.53 = (bf16[1,176,256]{2,1,0:T(8,128)(2,1)}, bf16[1,176,256]{2,1,0:T(8,128)(2,1)}, u32[]{:S(2)}, u32[]{:S(2)}) collective-permute-start(bf16[1,176,256]{2,1,0:T(8,128)(2,1)} %get-tuple-element.163), channel_id=1, source_target_pairs={{0,5},{1,4},{2,7},{3,6},{4,1},{5,0},{6,3},{7,2},{8,13},{9,12},{10,... | collective-permute-start | bytes 270344 | tf_op jit(solution)/shard_map/ppermute | solution.py:229
  331.4 18.1 %collective-permute-start.54 = (bf16[1,176,256]{2,1,0:T(8,128)(2,1)}, bf16[1,176,256]{2,1,0:T(8,128)(2,1)}, u32[]{:S(2)}, u32[]{:S(2)}) collective-permute-start(bf16[1,176,256]{2,1,0:T(8,128)(2,1)} %get-tuple-element.164), channel_id=1, source_target_pairs={{0,6},{1,7},{2,4},{3,5},{4,2},{5,3},{6,0},{7,1},{8,14},{9,15},{10,... | collective-permute-start | bytes 270344 | tf_op jit(solution)/shard_map/ppermute | solution.py:229
  (82 other events, 1113.5 us)

commit v2 on v1

--- a/solution.py
+++ b/solution.py
@@ -8,7 +8,8 @@
 
 SPAN = 248.0
 HALF = 124.0
-TINY = 1e-30
+TINY = 1.2e-19
+LEAST, RATE, DEEP = 0.05, 240.0 / 8.2, 120.0
 FAR = pl.BlockSpec(memory_space=pltpu.MemorySpace.HBM)
 
 
@@ -36,6 +37,10 @@
     return jnp.max(jnp.abs(x), axis=0, keepdims=True).astype(jnp.bfloat16).astype(jnp.float32)
 
 
+def offsets(n):
+    return (0, 2, 4, 6, 3, 5, 7, 1) if n == 8 else tuple(range(n))
+
+
 def encode_kernel(n, piece, *refs):
     x_ref = refs[0]
     outs, turned = refs[-1 - n : -1], refs[-1]
@@ -46,9 +51,9 @@
     y = jnp.exp2(jnp.abs(x) * step - HALF)
     y = jnp.where(x < 0, -y, y)
     turned[...] = y.astype(jnp.bfloat16).T
-    for o in range(n):
+    for k, o in enumerate(offsets(n)):
         first = pl.multiple_of((me ^ o) * piece, 16)
-        outs[o][0] = turned[pl.ds(first, piece), :]
+        outs[k][0] = turned[pl.ds(first, piece), :]
 
 
 def encode(x, first, count, n, after=()):
@@ -83,26 +88,29 @@
 
     @pl.when(e == experts - 1)
     def _():
-        total = sums[...]
-        high = total.astype(jnp.bfloat16).astype(jnp.float32)
-        rest = total - high
-        middle = rest.astype(jnp.bfloat16).astype(jnp.float32)
-        low = rest - middle
-        everything = jnp.concatenate([high, middle, low, tops[...]], axis=0)
-        turned[...] = everything.T.astype(jnp.bfloat16)
+        top = tops[...]
+        ratio = jnp.where(top > TINY, sums[...] / jnp.maximum(top * top, TINY * TINY), 1.0)
+        code = jnp.exp2((jnp.log2(ratio) + LEAST) * RATE - DEEP)
+        both = jnp.concatenate([code, top], axis=0)
+        turned[...] = jnp.concatenate([both, both], axis=0).T
         router = (router_ref[...] * gain_ref[...]).astype(jnp.bfloat16)
         half = router.shape[1] // 2
-        for o in range(n):
-            first = pl.multiple_of((me ^ o) * piece, 16)
-            outs[o][pl.ds(0, piece), :] = turned[pl.ds(first, piece), :]
-            outs[o][pl.ds(piece, experts), :] = router[:, :half]
-            outs[o][pl.ds(piece + experts, experts), :] = router[:, half:]
+        short = piece // 2
+        lane = lax.broadcasted_iota(jnp.int32, (short, 128), 1)
+        for k, o in enumerate(offsets(n)):
+            first = pl.multiple_of((me ^ o) * piece, 8)
+            one = turned[pl.ds(first, short), :]
+            two = turned[pl.ds(pl.multiple_of(first + short, 8), short), :]
+            outs[k][pl.ds(0, experts), :] = router[:, :half]
+            outs[k][pl.ds(experts, experts), :] = router[:, half:]
+            packed = jnp.where(lane < 64, one, two).astype(jnp.bfloat16)
+            outs[k][pl.ds(2 * experts, short), :] = packed
 
 
 def stats(gate, up, router, gain, n, after=()):
     experts, rows, cols = gate.shape
     piece = cols // n
-    block = jax.ShapeDtypeStruct((piece + 2 * experts, 128), jnp.bfloat16)
+    block = jax.ShapeDtypeStruct((piece // 2 + 2 * experts, 128), jnp.bfloat16)
     whole = pl.BlockSpec(memory_space=pltpu.VMEM)
     return pl.pallas_call(
         lambda *refs: stats_kernel(n, piece, experts, *refs),
@@ -116,7 +124,7 @@
         scratch_shapes=[
             pltpu.VMEM((2 * experts, cols), jnp.float32),
             pltpu.VMEM((2 * experts, cols), jnp.float32),
-            pltpu.VMEM((cols, 128), jnp.bfloat16),
+            pltpu.VMEM((cols, 128), jnp.float32),
         ],
         cost_estimate=pl.CostEstimate(
             flops=experts * 4_000_000, bytes_accessed=experts * rows * cols * 8, transcendentals=0
@@ -129,26 +137,29 @@
     factor_ref, gate_ref, up_ref, router_ref = refs[n:]
     me = lax.axis_index("shard")
     w = 2 * experts
-    half = rows // 2
+    half, short = rows // 2, piece // 2
     total, tops = None, []
-    for o in range(n):
-        lines = told[o][pl.ds(0, piece), :].astype(jnp.float32).T
-        part = lines[:w] + lines[w : 2 * w] + lines[2 * w : 3 * w]
+    for k, o in enumerate(offsets(n)):
+        lines = told[k][pl.ds(2 * experts, short), :].astype(jnp.float32).T
+        lines = jnp.concatenate([lines[: 2 * w], lines[2 * w :]], axis=1)
+        top = lines[w:]
+        ratio = jnp.exp2((jnp.log2(lines[:w]) + DEEP) / RATE - LEAST)
+        part = ratio * (top * top)
         total = part if total is None else total + part
-        tops.append(lines[3 * w : 4 * w])
-        for k in range(2):
-            at = pl.multiple_of((me ^ o) * rows + k * half, half)
-            router_ref[:, pl.ds(at, half)] = told[o][pl.ds(piece + k * experts, experts), :]
+        tops.append(top)
+        for h in range(2):
+            at = pl.multiple_of((me ^ o) * rows + h * half, half)
+            router_ref[:, pl.ds(at, half)] = told[k][pl.ds(h * experts, experts), :]
     scale = jnp.sqrt(total)
     gate_ref[...] = scale[:experts]
     up_ref[...] = scale[experts:]
-    for o in range(n):
-        factor_ref[:, o, :] = tops[o] / (SPAN * scale)
+    for k in range(n):
+        factor_ref[:, k, :] = tops[k] / (SPAN * scale)
 
 
 def factors(told, experts, rows, router_kind):
     n = len(told)
-    piece = told[0].shape[0] - 2 * experts
+    piece = 2 * (told[0].shape[0] - 2 * experts)
     return pl.pallas_call(
         lambda *refs: factor_kernel(n, piece, experts, rows, *refs),
         name="factors",
@@ -169,12 +180,15 @@
     token_ref[...] = jnp.zeros_like(token_ref)
     me = lax.axis_index("shard")
     factor = factor_ref[0].T
-    for o in range(n):
-        y = pieces[o][0].astype(jnp.float32)
-        v = (jnp.log2(jnp.abs(y)) + HALF) * factor[:, o : o + 1]
-        v = jnp.where(y < 0, -v, v).astype(jnp.bfloat16)
+    for k, o in enumerate(offsets(n)):
         first = pl.multiple_of((me ^ o) * rows, 128)
-        out_ref[0, :, pl.ds(first, rows)] = v
+        out_ref[0, :, pl.ds(first, rows)] = decoded(pieces[k][0], factor[:, k : k + 1])
+
+
+def decoded(y, factor):
+    y = y.astype(jnp.float32)
+    v = (jnp.log2(jnp.abs(y)) + HALF) * factor
+    return jnp.where(y < 0, -v, v).astype(jnp.bfloat16)
 
 
 def decode(pieces, factor, which, first, experts, into):
@@ -202,6 +216,53 @@
             flops=count * 4_000_000, bytes_accessed=count * rows * piece * n * 4, transcendentals=0
         ),
     )(factor, *pieces, *into)
+
+
+def finish_kernel(n, some, base, which, rows, *refs):
+    factor_ref, pieces = refs[0], refs[1 : 1 + len(some)]
+    out_ref, token_ref, ready, sems = refs[-4:]
+    token_ref[...] = jnp.zeros_like(token_ref)
+    me = lax.axis_index("shard")
+    factor = factor_ref[base].T
+    copies = []
+    for at, k in enumerate(some):
+        first = pl.multiple_of((me ^ offsets(n)[k]) * rows, 128)
+        ready[at] = decoded(pieces[at][0], factor[:, k : k + 1])
+        copies.append(
+            pltpu.make_async_copy(
+                ready.at[at], out_ref.at[which, :, pl.ds(first, rows)], sems.at[at]
+            )
+        )
+        copies[-1].start()
+    for copy in copies:
+        copy.wait()
+
+
+def finish(pieces, some, factor, base, which, into):
+    n = factor.shape[1]
+    _, piece, rows = pieces[0].shape
+    near = pl.BlockSpec(memory_space=pltpu.MemorySpace.VMEM)
+    return pl.pallas_call(
+        lambda *refs: finish_kernel(n, some, base, which, rows, *refs),
+        name="finish",
+        out_shape=[
+            jax.ShapeDtypeStruct(into.shape, into.dtype),
+            jax.ShapeDtypeStruct((8, 128), jnp.float32),
+        ],
+        in_specs=[near] * (1 + len(some)) + [FAR],
+        out_specs=[FAR, near],
+        scratch_shapes=[
+            pltpu.VMEM((len(some), piece, rows), jnp.bfloat16),
+            pltpu.SemaphoreType.DMA((len(some),)),
+        ],
+        input_output_aliases={len(some) + 1: 0},
+        compiler_params=pltpu.CompilerParams(vmem_limit_bytes=8 * 1024 * 1024),
+        cost_estimate=pl.CostEstimate(
+            flops=500_000 * len(some),
+            bytes_accessed=rows * piece * len(some) * 4,
+            transcendentals=0,
+        ),
+    )(factor, *pieces, into)
 
 
 def place_kernel(axis, along, n, part, *refs):
@@ -229,16 +290,11 @@
     return lax.ppermute(x, axis, [(i, i ^ o) for i in range(n)])
 
 
-ORDER = (2, 4, 6, 3, 5, 7, 1)
-
-
 def exchange(parts):
     n = len(parts)
-    got = [parts[0]] + [None] * (n - 1)
-    order = ORDER if n == 8 else range(1, n)
-    for o in order:
-        got[o] = swap(parts[o], "shard", n, o)
-    return got
+    return [parts[0]] + [
+        swap(parts[k], "shard", n, o) for k, o in enumerate(offsets(n)) if o
+    ]
 
 
 def cuts(experts):
@@ -252,7 +308,7 @@
 
 def plan(experts):
     if experts == 16:
-        sizes = ([2, 5, 5, 4], [5, 5, 5, 1])
+        sizes = ([2, 5, 5, 4], [5, 5, 3, 2, 1])
     else:
         sizes = (cuts(experts), cuts(experts))
     chunks = []
@@ -281,11 +337,21 @@
             after += tuple(got[k - AHEAD][1:])
         if k - AHEAD - 1 in tokens:
             after += (tokens[k - AHEAD - 1],)
+        if k == AHEAD + 3:
+            after += (placed,)
         sent = encode(source[which], first, size, n, after)
         got[k] = exchange(sent)
 
     def receive(k):
-        which, first, _ = chunks[k]
+        which, first, size = chunks[k]
+        if size == 1 and k == len(chunks) - 1:
+            base = which * experts + first
+            late = tuple(range(n // 2, n - 1))
+            soon = tuple(range(n // 2)) + (n - 1,)
+            for some in (soon, late):
+                pieces = [got[k][j] for j in some]
+                result[which], tokens[k] = finish(pieces, some, factor, base, first, result[which])
+            return
         result[which], tokens[k] = decode(
             got[k], factor, which, first, experts, result[which]
         )
@@ -298,7 +364,7 @@
     blocks = [rows_router] + [
         swap(rows_router, "expert", groups, o) for o in range(1, groups)
     ]
-    serve_router = place(blocks, "expert", 0).T
+    placed = place(blocks, "expert", 0)
     for k in range(AHEAD, len(chunks)):
         send(k)
         receive(k - AHEAD)
@@ -309,7 +375,7 @@
         result[1].transpose(0, 2, 1),
         scale_gate,
         scale_up,
-        serve_router,
+        placed.T,
     )
 
 

time: 355 us -> 319 us (0.90)
  waiting for transfers between devices: 165 us -> 98.5 us
  starting transfers between devices: 63.1 us -> 91.9 us
  Pallas kernels: 118 us -> 122 us
    ppermute x66 -> x73, waiting for transfers between devices: 165 us -> 98.5 us  [swap(): return lax.ppermute(x, axis, [(i, i ^ o) for i in range(n)])]
    ppermute x66 -> x73, starting transfers between devices: 63.1 us -> 91.9 us  [swap(): return lax.ppermute(x, axis, [(i, i ^ o) for i in range(n)])]
    pallas_call x8 -> x9, Pallas kernels: 49.3 us -> 50.8 us  [encode(): pl.pallas_call(lambda *refs: encode_kernel(n, piece, *refs), name='encode...]
  transfers between devices with their start and end apart: 66 -> 73, of which waited for: 19 -> 23; matrix products, arithmetic and copies ran while one was open for 0% -> 0% of each run, Pallas kernels for 27% -> 32%
where the time goes in v2:
time: 319 us; the launch traced here: 316 us
  Pallas kernels  122 us (38%)
  waiting for transfers between devices  98.5 us (31%)
  starting transfers between devices  91.9 us (29%)
    ppermute x73, waiting for transfers between devices, swap(): return lax.ppermute(x, axis, [(i, i ^ o) for i in range(n)])  98.5 us
    ppermute x73, starting transfers between devices, swap(): return lax.ppermute(x, axis, [(i, i ^ o) for i in range(n)])  91.9 us
    pallas_call x9, Pallas kernels, encode(): pl.pallas_call(lambda *refs: encode_kernel(n, piece, *refs), name='encode...  50.8 us
    pallas_call x8, Pallas kernels, decode(): pl.pallas_call(lambda *refs: decode_kernel(n, rows, *refs), name='decode'...  44 us
    pallas_call x1, Pallas kernels, stats(): pl.pallas_call(lambda *refs: stats_kernel(n, piece, experts, *refs), name...  20.3 us
  transfers between devices with their start and end apart: 73, of which 23 were waited for; matrix products, arithmetic and copies ran while one was open for 0% of the time, Pallas kernels for 32%

profile of v2, /device:TPU:0, one launch (start us, length us, event | category | flops | bytes accessed | tf_op | source)
XLA Modules:
  0.0 316.0 jit_solution(3978730128632473719)
XLA Ops:
  0.6 20.3 %stats.1 = (bf16[120,128]{1,0:T(8,128)(2,1)}, bf16[120,128]{1,0:T(8,128)(2,1)}, bf16[120,128]{1,0:T(8,128)(2,1)}, bf16[120,128]{1,0:T(8,128)(2,1)}, bf16[120,128...) custom-call(f32[16,256,1408]{2,1,0:T(8,128)} %refs_0_.14, ...), custom_call_target="tpu_custom_call" | custom-call | flops 64000000 | bytes 46137344 | tf_op jit(solution)/shard_map/stats/pallas_call | solution.py:115
  20.9 3.0 collective-permute-start
  25.6 3.4 %encode.10 = (bf16[2,176,256]{2,1,0:T(8,128)(2,1)}, bf16[2,176,256]{2,1,0:T(8,128)(2,1)}, bf16[2,176,256]{2,1,0:T(8,128)(2,1)}, bf16[2,176,256]{2,1,0:T(8,128)(2...) custom-call(f32[16,256,1408]{2,1,0:T(8,128)} %refs_0_.14), custom_call_target="tpu_custom_call" | custom-call | flops 8000000 | bytes 4325376 | tf_op jit(solution)/shard_map/encode/pallas_call | solution.py:63
  29.0 2.0 collective-permute-start.14
  31.0 1.8 collective-permute-start.4
  34.8 2.6 collective-permute-done.5.refs_6_
  38.0 1.9 factors.1
  40.0 3.6 %collective-permute-start.51 = (bf16[16,2048]{1,0:T(8,128)(2,1)}, bf16[16,2048]{1,0:T(8,128)(2,1)S(1)}, u32[]{:S(2)}, u32[]{:S(2)}) collective-permute-start(bf16[16,2048]{1,0:T(8,128)(2,1)} %get-tuple-element.168.refs_0_), channel_id=1, source_target_pairs={{0,24},{8,16},{16,8},{24,0},{1,25},{9,17},{17,9},{25,1},{2,26},{10... | collective-permute-start | bytes 196616 | tf_op jit(solution)/shard_map/ppermute | solution.py:290
  44.0 2.5 collective-permute-start.16
  47.4 4.5 %collective-permute-done.50.refs_2_ = bf16[16,2048]{1,0:T(8,128)(2,1)S(1)} collective-permute-done((bf16[16,2048]{1,0:T(8,128)(2,1)}, bf16[16,2048]{1,0:T(8,128)(2,1)S(1)}, u32[]{:S(2)}, u32[]{:S(2)}) %collective-permute-start.50) | collective-permute-done | bytes 65568 | tf_op jit(solution)/shard_map/ppermute | solution.py:290
  54.4 7.4 %encode.9 = (bf16[5,176,256]{2,1,0:T(8,128)(2,1)}, bf16[5,176,256]{2,1,0:T(8,128)(2,1)}, bf16[5,176,256]{2,1,0:T(8,128)(2,1)}, bf16[5,176,256]{2,1,0:T(8,128)(2,...) custom-call(f32[16,256,1408]{2,1,0:T(8,128)} %refs_0_.14), custom_call_target="tpu_custom_call" | custom-call | flops 20000000 | bytes 10813440 | tf_op jit(solution)/shard_map/encode/pallas_call | solution.py:63
  68.7 6.2 %collective-permute-done.7.refs_1_.refs_2_ = bf16[5,176,256]{2,1,0:T(8,128)(2,1)S(1)} collective-permute-done((bf16[5,176,256]{2,1,0:T(8,128)(2,1)}, bf16[5,176,256]{2,1,0:T(8,128)(2,1)S(1)}, u32[]{:S(2)}, u32[]{:S(2)}) %collective-permute-start.7) | collective-permute-done | bytes 450592 | tf_op jit(solution)/shard_map/ppermute | solution.py:290
  75.6 10.8 %collective-permute-done.8.refs_2_.refs_3_ = bf16[5,176,256]{2,1,0:T(8,128)(2,1)S(1)} collective-permute-done((bf16[5,176,256]{2,1,0:T(8,128)(2,1)}, bf16[5,176,256]{2,1,0:T(8,128)(2,1)S(1)}, u32[]{:S(2)}, u32[]{:S(2)}) %collective-permute-start.8) | collective-permute-done | bytes 450592 | tf_op jit(solution)/shard_map/ppermute | solution.py:290
  86.5 7.5 %encode.12 = (bf16[5,176,256]{2,1,0:T(8,128)(2,1)}, bf16[5,176,256]{2,1,0:T(8,128)(2,1)}, bf16[5,176,256]{2,1,0:T(8,128)(2,1)}, bf16[5,176,256]{2,1,0:T(8,128)(2...) custom-call(f32[16,256,1408]{2,1,0:T(8,128)} %refs_0_.14, ...), custom_call_target="tpu_custom_call" | custom-call | flops 20000000 | bytes 10813440 | tf_op jit(solution)/shard_map/encode/pallas_call | solution.py:63
  96.1 8.9 %collective-permute-start.30 = (bf16[5,176,256]{2,1,0:T(8,128)(2,1)}, bf16[5,176,256]{2,1,0:T(8,128)(2,1)S(1)}, u32[]{:S(2)}, u32[]{:S(2)}) collective-permute-start(bf16[5,176,256]{2,1,0:T(8,128)(2,1)} %get-tuple-element.141), channel_id=1, source_target_pairs={{0,6},{1,7},{2,4},{3,5},{4,2},{5,3},{6,0},{7,1},{8,14},{9,15},{10,... | collective-permute-start | bytes 1351688 | tf_op jit(solution)/shard_map/ppermute | solution.py:290
  107.2 6.4 %collective-permute-done.28.refs_2_.refs_1_ = bf16[5,176,256]{2,1,0:T(8,128)(2,1)S(1)} collective-permute-done((bf16[5,176,256]{2,1,0:T(8,128)(2,1)}, bf16[5,176,256]{2,1,0:T(8,128)(2,1)S(1)}, u32[]{:S(2)}, u32[]{:S(2)}) %collective-permute-start.28) | collective-permute-done | bytes 450592 | tf_op jit(solution)/shard_map/ppermute | solution.py:290
  114.3 10.6 %collective-permute-done.29.refs_3_.refs_2_ = bf16[5,176,256]{2,1,0:T(8,128)(2,1)S(1)} collective-permute-done((bf16[5,176,256]{2,1,0:T(8,128)(2,1)}, bf16[5,176,256]{2,1,0:T(8,128)(2,1)S(1)}, u32[]{:S(2)}, u32[]{:S(2)}) %collective-permute-start.29) | collective-permute-done | bytes 450592 | tf_op jit(solution)/shard_map/ppermute | solution.py:290
  124.9 3.4 %decode.8 = (bf16[16,176,2048]{2,1,0:T(8,128)(2,1)}, f32[8,128]{1,0:T(8,128)}) custom-call(f32[32,8,176]{2,1,0:T(8,128)} %get-tuple-element.113.refs_0_, bf16[2,176,256]{2,1,0:T(8,128)(2,1)} %get-tuple-element.121.refs_1_, bf16[2,176,256]{2,1,0:T(8,128)(2,1)} %copy-done.34, bf16[2,176,256]{2,1,0:T(8,128)(2,1)} %copy-done.35, ...), custom_call_target="tpu_custom_call" | custom-call | flops 8000000 | bytes 2883584 | tf_op jit(solution)/shard_map/decode/pallas_call | solution.py:199
  128.3 5.8 %encode.11 = (bf16[4,176,256]{2,1,0:T(8,128)(2,1)}, bf16[4,176,256]{2,1,0:T(8,128)(2,1)}, bf16[4,176,256]{2,1,0:T(8,128)(2,1)}, bf16[4,176,256]{2,1,0:T(8,128)(2...) custom-call(f32[16,256,1408]{2,1,0:T(8,128)} %refs_0_.14, ...), custom_call_target="tpu_custom_call" | custom-call | flops 16000000 | bytes 8650752 | tf_op jit(solution)/shard_map/encode/pallas_call | solution.py:63
  135.2 8.4 %collective-permute-start.23 = (bf16[4,176,256]{2,1,0:T(8,128)(2,1)}, bf16[4,176,256]{2,1,0:T(8,128)(2,1)S(1)}, u32[]{:S(2)}, u32[]{:S(2)}) collective-permute-start(bf16[4,176,256]{2,1,0:T(8,128)(2,1)} %get-tuple-element.133), channel_id=1, source_target_pairs={{0,6},{1,7},{2,4},{3,5},{4,2},{5,3},{6,0},{7,1},{8,14},{9,15},{10,... | collective-permute-start | bytes 1081352 | tf_op jit(solution)/shard_map/ppermute | solution.py:290
  145.8 4.6 %collective-permute-done.21.refs_2_.refs_1_ = bf16[4,176,256]{2,1,0:T(8,128)(2,1)S(1)} collective-permute-done((bf16[4,176,256]{2,1,0:T(8,128)(2,1)}, bf16[4,176,256]{2,1,0:T(8,128)(2,1)S(1)}, u32[]{:S(2)}, u32[]{:S(2)}) %collective-permute-start.21) | collective-permute-done | bytes 360480 | tf_op jit(solution)/shard_map/ppermute | solution.py:290
  151.1 6.7 %decode.9 = (bf16[16,176,2048]{2,1,0:T(8,128)(2,1)}, f32[8,128]{1,0:T(8,128)}) custom-call(f32[32,8,176]{2,1,0:T(8,128)} %get-tuple-element.113.refs_0_, bf16[5,176,256]{2,1,0:T(8,128)(2,1)} %get-tuple-element.146.refs_1_, bf16[5,176,256]{2,1,0:T(8,128)(2,1)} %copy-done.13, bf16[5,176,256]{2,1,0:T(8,128)(2,1)} %copy-done.15, ...), custom_call_target="tpu_custom_call", output_to_operand_aliasing={{0}: (9, {})} | custom-call | flops 20000000 | bytes 7208960 | tf_op jit(solution)/shard_map/decode/pallas_call | solution.py:199
  157.8 7.5 %encode.13 = (bf16[5,176,256]{2,1,0:T(8,128)(2,1)}, bf16[5,176,256]{2,1,0:T(8,128)(2,1)}, bf16[5,176,256]{2,1,0:T(8,128)(2,1)}, bf16[5,176,256]{2,1,0:T(8,128)(2...) custom-call(f32[16,256,1408]{2,1,0:T(8,128)} %refs_0_.19, ...), custom_call_target="tpu_custom_call" | custom-call | flops 20000000 | bytes 10813440 | tf_op jit(solution)/shard_map/encode/pallas_call | solution.py:63
  169.7 4.7 %collective-permute-start.37 = (bf16[5,176,256]{2,1,0:T(8,128)(2,1)}, bf16[5,176,256]{2,1,0:T(8,128)(2,1)S(1)}, u32[]{:S(2)}, u32[]{:S(2)}) collective-permute-start(bf16[5,176,256]{2,1,0:T(8,128)(2,1)} %get-tuple-element.154), channel_id=1, source_target_pairs={{0,6},{1,7},{2,4},{3,5},{4,2},{5,3},{6,0},{7,1},{8,14},{9,15},{10,... | collective-permute-start | bytes 1351688 | tf_op jit(solution)/shard_map/ppermute | solution.py:290
  176.7 6.6 %collective-permute-done.35.refs_1_.refs_2_ = bf16[5,176,256]{2,1,0:T(8,128)(2,1)S(1)} collective-permute-done((bf16[5,176,256]{2,1,0:T(8,128)(2,1)}, bf16[5,176,256]{2,1,0:T(8,128)(2,1)S(1)}, u32[]{:S(2)}, u32[]{:S(2)}) %collective-permute-start.35) | collective-permute-done | bytes 450592 | tf_op jit(solution)/shard_map/ppermute | solution.py:290
  185.7 6.7 %decode.10 = (bf16[16,176,2048]{2,1,0:T(8,128)(2,1)}, f32[8,128]{1,0:T(8,128)}) custom-call(f32[32,8,176]{2,1,0:T(8,128)} %get-tuple-element.113.refs_0_, bf16[5,176,256]{2,1,0:T(8,128)(2,1)} %get-tuple-element.138.refs_1_, bf16[5,176,256]{2,1,0:T(8,128)(2,1)} %copy-done.10, bf16[5,176,256]{2,1,0:T(8,128)(2,1)} %copy-done.12, ...), custom_call_target="tpu_custom_call", output_to_operand_aliasing={{0}: (9, {})} | custom-call | flops 20000000 | bytes 7208960 | tf_op jit(solution)/shard_map/decode/pallas_call | solution.py:199
  192.4 1.7 collective-permute-done.36.refs_2_.refs_3_
  194.2 7.6 %encode.15 = (bf16[5,176,256]{2,1,0:T(8,128)(2,1)}, bf16[5,176,256]{2,1,0:T(8,128)(2,1)}, bf16[5,176,256]{2,1,0:T(8,128)(2,1)}, bf16[5,176,256]{2,1,0:T(8,128)(2...) custom-call(f32[16,256,1408]{2,1,0:T(8,128)} %refs_0_.19, ...), custom_call_target="tpu_custom_call" | custom-call | flops 20000000 | bytes 10813440 | tf_op jit(solution)/shard_map/encode/pallas_call | solution.py:63
  204.0 8.9 %collective-permute-start.54 = (bf16[5,176,256]{2,1,0:T(8,128)(2,1)}, bf16[5,176,256]{2,1,0:T(8,128)(2,1)}, u32[]{:S(2)}, u32[]{:S(2)}) collective-permute-start(bf16[5,176,256]{2,1,0:T(8,128)(2,1)} %get-tuple-element.172), channel_id=1, source_target_pairs={{0,6},{1,7},{2,4},{3,5},{4,2},{5,3},{6,0},{7,1},{8,14},{9,15},{10,... | collective-permute-start | bytes 1351688 | tf_op jit(solution)/shard_map/ppermute | solution.py:290
  215.3 6.7 %collective-permute-done.52.refs_2_.refs_1_ = bf16[5,176,256]{2,1,0:T(8,128)(2,1)S(1)} collective-permute-done((bf16[5,176,256]{2,1,0:T(8,128)(2,1)}, bf16[5,176,256]{2,1,0:T(8,128)(2,1)S(1)}, u32[]{:S(2)}, u32[]{:S(2)}) %collective-permute-start.52) | collective-permute-done | bytes 450592 | tf_op jit(solution)/shard_map/ppermute | solution.py:290
  222.7 9.8 %collective-permute-done.53.refs_3_.refs_2_ = bf16[5,176,256]{2,1,0:T(8,128)(2,1)S(1)} collective-permute-done((bf16[5,176,256]{2,1,0:T(8,128)(2,1)}, bf16[5,176,256]{2,1,0:T(8,128)(2,1)S(1)}, u32[]{:S(2)}, u32[]{:S(2)}) %collective-permute-start.53) | collective-permute-done | bytes 450592 | tf_op jit(solution)/shard_map/ppermute | solution.py:290
  232.5 5.5 %decode.11 = (bf16[16,176,2048]{2,1,0:T(8,128)(2,1)}, f32[8,128]{1,0:T(8,128)}) custom-call(f32[32,8,176]{2,1,0:T(8,128)} %get-tuple-element.113.refs_0_, bf16[4,176,256]{2,1,0:T(8,128)(2,1)} %get-tuple-element.130.refs_1_, bf16[4,176,256]{2,1,0:T(8,128)(2,1)} %copy-done.21, bf16[4,176,256]{2,1,0:T(8,128)(2,1)} %copy-done.22, ...), custom_call_target="tpu_custom_call", output_to_operand_aliasing={{0}: (9, {})} | custom-call | flops 16000000 | bytes 5767168 | tf_op jit(solution)/shard_map/decode/pallas_call | solution.py:199
  238.0 5.3 %encode.14 = (bf16[3,176,256]{2,1,0:T(8,128)(2,1)}, bf16[3,176,256]{2,1,0:T(8,128)(2,1)}, bf16[3,176,256]{2,1,0:T(8,128)(2,1)}, bf16[3,176,256]{2,1,0:T(8,128)(2...) custom-call(f32[16,256,1408]{2,1,0:T(8,128)} %refs_0_.19, ...), custom_call_target="tpu_custom_call" | custom-call | flops 12000000 | bytes 6488064 | tf_op jit(solution)/shard_map/encode/pallas_call | solution.py:63
  245.0 2.0 collective-permute-start.44
  246.9 4.4 %collective-permute-done.57.refs_7_.refs_6_ = bf16[5,176,256]{2,1,0:T(8,128)(2,1)} collective-permute-done((bf16[5,176,256]{2,1,0:T(8,128)(2,1)}, bf16[5,176,256]{2,1,0:T(8,128)(2,1)}, u32[]{:S(2)}, u32[]{:S(2)}) %collective-permute-start.57) | collective-permute-done | bytes 450592 | tf_op jit(solution)/shard_map/ppermute | solution.py:290
  253.9 2.9 collective-permute-done.42.refs_1_.refs_2_
  257.6 5.6 %collective-permute-done.43.refs_2_.refs_3_ = bf16[3,176,256]{2,1,0:T(8,128)(2,1)S(1)} collective-permute-done((bf16[3,176,256]{2,1,0:T(8,128)(2,1)}, bf16[3,176,256]{2,1,0:T(8,128)(2,1)S(1)}, u32[]{:S(2)}, u32[]{:S(2)}) %collective-permute-start.43) | collective-permute-done | bytes 270368 | tf_op jit(solution)/shard_map/ppermute | solution.py:290
  263.2 6.8 %decode.12 = (bf16[16,176,2048]{2,1,0:T(8,128)(2,1)}, f32[8,128]{1,0:T(8,128)}) custom-call(f32[32,8,176]{2,1,0:T(8,128)} %get-tuple-element.113.refs_0_, bf16[5,176,256]{2,1,0:T(8,128)(2,1)} %get-tuple-element.177.refs_1_, bf16[5,176,256]{2,1,0:T(8,128)(2,1)} %copy-done.2, bf16[5,176,256]{2,1,0:T(8,128)(2,1)} %copy-done.3, bf16[5,176,256]{2,1,0:T(8,128)(2,1)} %copy-done.4, ...), custom_call_target="tpu_custom_call" | custom-call | flops 20000000 | bytes 7208960 | tf_op jit(solution)/shard_map/decode/pallas_call | solution.py:199
  270.0 3.5 %encode.17 = (bf16[2,176,256]{2,1,0:T(8,128)(2,1)}, bf16[2,176,256]{2,1,0:T(8,128)(2,1)}, bf16[2,176,256]{2,1,0:T(8,128)(2,1)}, bf16[2,176,256]{2,1,0:T(8,128)(2...) custom-call(f32[16,256,1408]{2,1,0:T(8,128)} %refs_0_.19, ...), custom_call_target="tpu_custom_call" | custom-call | flops 8000000 | bytes 4325376 | tf_op jit(solution)/shard_map/encode/pallas_call | solution.py:63
  273.5 1.8 collective-permute-start.66
  278.6 2.6 collective-permute-done.66.refs_2_
  281.2 6.2 %collective-permute-done.67.refs_3_ = bf16[2,176,256]{2,1,0:T(8,128)(2,1)S(1)} collective-permute-done((bf16[2,176,256]{2,1,0:T(8,128)(2,1)}, bf16[2,176,256]{2,1,0:T(8,128)(2,1)S(1)}, u32[]{:S(2)}, u32[]{:S(2)}) %collective-permute-start.67) | collective-permute-done | bytes 180256 | tf_op jit(solution)/shard_map/ppermute | solution.py:290
  287.4 6.8 %decode.13 = (bf16[16,176,2048]{2,1,0:T(8,128)(2,1)}, f32[8,128]{1,0:T(8,128)}) custom-call(f32[32,8,176]{2,1,0:T(8,128)} %get-tuple-element.113.refs_0_, bf16[5,176,256]{2,1,0:T(8,128)(2,1)} %get-tuple-element.169.refs_1_, bf16[5,176,256]{2,1,0:T(8,128)(2,1)} %copy-done.9, bf16[5,176,256]{2,1,0:T(8,128)(2,1)} %copy-done.11, ...), custom_call_target="tpu_custom_call", output_to_operand_aliasing={{0}: (9, {})} | custom-call | flops 20000000 | bytes 7208960 | tf_op jit(solution)/shard_map/decode/pallas_call | solution.py:199
  294.2 2.8 encode.16
  297.3 3.4 %collective-permute-start.64 = (bf16[1,176,256]{2,1,0:T(8,128)(2,1)}, bf16[1,176,256]{2,1,0:T(8,128)(2,1)S(1)}, u32[]{:S(2)}, u32[]{:S(2)}) collective-permute-start(bf16[1,176,256]{2,1,0:T(8,128)(2,1)} %get-tuple-element.186), channel_id=1, source_target_pairs={{0,6},{1,7},{2,4},{3,5},{4,2},{5,3},{6,0},{7,1},{8,14},{9,15},{10,... | collective-permute-start | bytes 270344 | tf_op jit(solution)/shard_map/ppermute | solution.py:290
  300.9 2.0 collective-permute-done.62.refs_2_
  304.4 4.8 %decode.14 = (bf16[16,176,2048]{2,1,0:T(8,128)(2,1)}, f32[8,128]{1,0:T(8,128)}) custom-call(f32[32,8,176]{2,1,0:T(8,128)} %get-tuple-element.113.refs_0_, bf16[3,176,256]{2,1,0:T(8,128)(2,1)} %get-tuple-element.197.refs_1_, bf16[3,176,256]{2,1,0:T(8,128)(2,1)} %copy-done.27, bf16[3,176,256]{2,1,0:T(8,128)(2,1)} %copy-done.28, ...), custom_call_target="tpu_custom_call", output_to_operand_aliasing={{0}: (9, {})} | custom-call | flops 12000000 | bytes 4325376 | tf_op jit(solution)/shard_map/decode/pallas_call | solution.py:199
  309.2 3.3 %decode.15 = (bf16[16,176,2048]{2,1,0:T(8,128)(2,1)}, f32[8,128]{1,0:T(8,128)}) custom-call(f32[32,8,176]{2,1,0:T(8,128)} %get-tuple-element.113.refs_0_, bf16[2,176,256]{2,1,0:T(8,128)(2,1)} %get-tuple-element.189.refs_1_, bf16[2,176,256]{2,1,0:T(8,128)(2,1)} %copy-done.41, bf16[2,176,256]{2,1,0:T(8,128)(2,1)} %copy-done.42, ...), custom_call_target="tpu_custom_call", output_to_operand_aliasing={{0}: (9, {})} | custom-call | flops 8000000 | bytes 2883584 | tf_op jit(solution)/shard_map/decode/pallas_call | solution.py:199
  (246 shorter events, 52.4 us)
Async XLA Ops:
  29.0 24.4 %collective-permute-start.14 = (bf16[2,176,256]{2,1,0:T(8,128)(2,1)}, bf16[2,176,256]{2,1,0:T(8,128)(2,1)S(1)}, u32[]{:S(2)}, u32[]{:S(2)}) collective-permute-start(bf16[2,176,256]{2,1,0:T(8,128)(2,1)} %get-tuple-element.122), channel_id=1, source_target_pairs={{0,2},{1,3},{2,0},{3,1},{4,6},{5,7},{6,4},{7,5},{8,10},{9,11},{10,... | collective-permute-start | bytes 540680 | tf_op jit(solution)/shard_map/ppermute | solution.py:290
  43.6 18.3 %collective-permute-start.15 = (bf16[2,176,256]{2,1,0:T(8,128)(2,1)}, bf16[2,176,256]{2,1,0:T(8,128)(2,1)S(1)}, u32[]{:S(2)}, u32[]{:S(2)}) collective-permute-start(bf16[2,176,256]{2,1,0:T(8,128)(2,1)} %get-tuple-element.123), channel_id=1, source_target_pairs={{0,4},{1,5},{2,6},{3,7},{4,0},{5,1},{6,2},{7,3},{8,12},{9,13},{10,... | collective-permute-start | bytes 540680 | tf_op jit(solution)/shard_map/ppermute | solution.py:290
  44.0 19.3 %collective-permute-start.16 = (bf16[2,176,256]{2,1,0:T(8,128)(2,1)}, bf16[2,176,256]{2,1,0:T(8,128)(2,1)S(1)}, u32[]{:S(2)}, u32[]{:S(2)}) collective-permute-start(bf16[2,176,256]{2,1,0:T(8,128)(2,1)} %get-tuple-element.124), channel_id=1, source_target_pairs={{0,6},{1,7},{2,4},{3,5},{4,2},{5,3},{6,0},{7,1},{8,14},{9,15},{10,... | collective-permute-start | bytes 540680 | tf_op jit(solution)/shard_map/ppermute | solution.py:290
  63.3 23.1 %collective-permute-start.8 = (bf16[5,176,256]{2,1,0:T(8,128)(2,1)}, bf16[5,176,256]{2,1,0:T(8,128)(2,1)S(1)}, u32[]{:S(2)}, u32[]{:S(2)}) collective-permute-start(bf16[5,176,256]{2,1,0:T(8,128)(2,1)} %get-tuple-element.115), channel_id=1, source_target_pairs={{0,4},{1,5},{2,6},{3,7},{4,0},{5,1},{6,2},{7,3},{8,12},{9,13},{10,... | collective-permute-start | bytes 1351688 | tf_op jit(solution)/shard_map/ppermute | solution.py:290
  64.0 30.0 %collective-permute-start.9 = (bf16[5,176,256]{2,1,0:T(8,128)(2,1)}, bf16[5,176,256]{2,1,0:T(8,128)(2,1)S(1)}, u32[]{:S(2)}, u32[]{:S(2)}) collective-permute-start(bf16[5,176,256]{2,1,0:T(8,128)(2,1)} %get-tuple-element.116), channel_id=1, source_target_pairs={{0,6},{1,7},{2,4},{3,5},{4,2},{5,3},{6,0},{7,1},{8,14},{9,15},{10,... | collective-permute-start | bytes 1351688 | tf_op jit(solution)/shard_map/ppermute | solution.py:290
  65.4 29.7 %collective-permute-start.10 = (bf16[5,176,256]{2,1,0:T(8,128)(2,1)}, bf16[5,176,256]{2,1,0:T(8,128)(2,1)S(1)}, u32[]{:S(2)}, u32[]{:S(2)}) collective-permute-start(bf16[5,176,256]{2,1,0:T(8,128)(2,1)} %get-tuple-element.117), channel_id=1, source_target_pairs={{0,3},{1,2},{2,1},{3,0},{4,7},{5,6},{6,5},{7,4},{8,11},{9,10},{10,... | collective-permute-start | bytes 1351688 | tf_op jit(solution)/shard_map/ppermute | solution.py:290
  68.1 28.1 %collective-permute-start.11 = (bf16[5,176,256]{2,1,0:T(8,128)(2,1)}, bf16[5,176,256]{2,1,0:T(8,128)(2,1)S(1)}, u32[]{:S(2)}, u32[]{:S(2)}) collective-permute-start(bf16[5,176,256]{2,1,0:T(8,128)(2,1)} %get-tuple-element.118), channel_id=1, source_target_pairs={{0,5},{1,4},{2,7},{3,6},{4,1},{5,0},{6,3},{7,2},{8,13},{9,12},{10,... | collective-permute-start | bytes 1351688 | tf_op jit(solution)/shard_map/ppermute | solution.py:290
  74.9 30.1 %collective-permute-start.12 = (bf16[5,176,256]{2,1,0:T(8,128)(2,1)}, bf16[5,176,256]{2,1,0:T(8,128)(2,1)}, u32[]{:S(2)}, u32[]{:S(2)}) collective-permute-start(bf16[5,176,256]{2,1,0:T(8,128)(2,1)} %get-tuple-element.119), channel_id=1, source_target_pairs={{0,7},{1,6},{2,5},{3,4},{4,3},{5,2},{6,1},{7,0},{8,15},{9,14},{10,... | collective-permute-start | bytes 1351688 | tf_op jit(solution)/shard_map/ppermute | solution.py:290
  86.4 19.6 %collective-permute-start.13 = (bf16[5,176,256]{2,1,0:T(8,128)(2,1)}, bf16[5,176,256]{2,1,0:T(8,128)(2,1)}, u32[]{:S(2)}, u32[]{:S(2)}) collective-permute-start(bf16[5,176,256]{2,1,0:T(8,128)(2,1)} %get-tuple-element.120), channel_id=1, source_target_pairs={{0,1},{1,0},{2,3},{3,2},{4,5},{5,4},{6,7},{7,6},{8,9},{9,8},{10,11... | collective-permute-start | bytes 1351688 | tf_op jit(solution)/shard_map/ppermute | solution.py:290
  94.0 19.6 %collective-permute-start.28 = (bf16[5,176,256]{2,1,0:T(8,128)(2,1)}, bf16[5,176,256]{2,1,0:T(8,128)(2,1)S(1)}, u32[]{:S(2)}, u32[]{:S(2)}) collective-permute-start(bf16[5,176,256]{2,1,0:T(8,128)(2,1)} %get-tuple-element.139), channel_id=1, source_target_pairs={{0,2},{1,3},{2,0},{3,1},{4,6},{5,7},{6,4},{7,5},{8,10},{9,11},{10,... | collective-permute-start | bytes 1351688 | tf_op jit(solution)/shard_map/ppermute | solution.py:290
  95.2 29.7 %collective-permute-start.29 = (bf16[5,176,256]{2,1,0:T(8,128)(2,1)}, bf16[5,176,256]{2,1,0:T(8,128)(2,1)S(1)}, u32[]{:S(2)}, u32[]{:S(2)}) collective-permute-start(bf16[5,176,256]{2,1,0:T(8,128)(2,1)} %get-tuple-element.140), channel_id=1, source_target_pairs={{0,4},{1,5},{2,6},{3,7},{4,0},{5,1},{6,2},{7,3},{8,12},{9,13},{10,... | collective-permute-start | bytes 1351688 | tf_op jit(solution)/shard_map/ppermute | solution.py:290
  96.1 38.0 %collective-permute-start.30 = (bf16[5,176,256]{2,1,0:T(8,128)(2,1)}, bf16[5,176,256]{2,1,0:T(8,128)(2,1)S(1)}, u32[]{:S(2)}, u32[]{:S(2)}) collective-permute-start(bf16[5,176,256]{2,1,0:T(8,128)(2,1)} %get-tuple-element.141), channel_id=1, source_target_pairs={{0,6},{1,7},{2,4},{3,5},{4,2},{5,3},{6,0},{7,1},{8,14},{9,15},{10,... | collective-permute-start | bytes 1351688 | tf_op jit(solution)/shard_map/ppermute | solution.py:290
  105.0 30.1 %collective-permute-start.31 = (bf16[5,176,256]{2,1,0:T(8,128)(2,1)}, bf16[5,176,256]{2,1,0:T(8,128)(2,1)S(1)}, u32[]{:S(2)}, u32[]{:S(2)}) collective-permute-start(bf16[5,176,256]{2,1,0:T(8,128)(2,1)} %get-tuple-element.142), channel_id=1, source_target_pairs={{0,3},{1,2},{2,1},{3,0},{4,7},{5,6},{6,5},{7,4},{8,11},{9,10},{10,... | collective-permute-start | bytes 1351688 | tf_op jit(solution)/shard_map/ppermute | solution.py:290
  106.0 29.2 %collective-permute-start.32 = (bf16[5,176,256]{2,1,0:T(8,128)(2,1)}, bf16[5,176,256]{2,1,0:T(8,128)(2,1)S(1)}, u32[]{:S(2)}, u32[]{:S(2)}) collective-permute-start(bf16[5,176,256]{2,1,0:T(8,128)(2,1)} %get-tuple-element.143), channel_id=1, source_target_pairs={{0,5},{1,4},{2,7},{3,6},{4,1},{5,0},{6,3},{7,2},{8,13},{9,12},{10,... | collective-permute-start | bytes 1351688 | tf_op jit(solution)/shard_map/ppermute | solution.py:290
  113.6 30.0 %collective-permute-start.33 = (bf16[5,176,256]{2,1,0:T(8,128)(2,1)}, bf16[5,176,256]{2,1,0:T(8,128)(2,1)}, u32[]{:S(2)}, u32[]{:S(2)}) collective-permute-start(bf16[5,176,256]{2,1,0:T(8,128)(2,1)} %get-tuple-element.144), channel_id=1, source_target_pairs={{0,7},{1,6},{2,5},{3,4},{4,3},{5,2},{6,1},{7,0},{8,15},{9,14},{10,... | collective-permute-start | bytes 1351688 | tf_op jit(solution)/shard_map/ppermute | solution.py:290
  124.9 19.7 %collective-permute-start.34 = (bf16[5,176,256]{2,1,0:T(8,128)(2,1)}, bf16[5,176,256]{2,1,0:T(8,128)(2,1)}, u32[]{:S(2)}, u32[]{:S(2)}) collective-permute-start(bf16[5,176,256]{2,1,0:T(8,128)(2,1)} %get-tuple-element.145), channel_id=1, source_target_pairs={{0,1},{1,0},{2,3},{3,2},{4,5},{5,4},{6,7},{7,6},{8,9},{9,8},{10,11... | collective-permute-start | bytes 1351688 | tf_op jit(solution)/shard_map/ppermute | solution.py:290
  134.2 16.2 %collective-permute-start.21 = (bf16[4,176,256]{2,1,0:T(8,128)(2,1)}, bf16[4,176,256]{2,1,0:T(8,128)(2,1)S(1)}, u32[]{:S(2)}, u32[]{:S(2)}) collective-permute-start(bf16[4,176,256]{2,1,0:T(8,128)(2,1)} %get-tuple-element.131), channel_id=1, source_target_pairs={{0,2},{1,3},{2,0},{3,1},{4,6},{5,7},{6,4},{7,5},{8,10},{9,11},{10,... | collective-permute-start | bytes 1081352 | tf_op jit(solution)/shard_map/ppermute | solution.py:290
  135.2 30.2 %collective-permute-start.22 = (bf16[4,176,256]{2,1,0:T(8,128)(2,1)}, bf16[4,176,256]{2,1,0:T(8,128)(2,1)S(1)}, u32[]{:S(2)}, u32[]{:S(2)}) collective-permute-start(bf16[4,176,256]{2,1,0:T(8,128)(2,1)} %get-tuple-element.132), channel_id=1, source_target_pairs={{0,4},{1,5},{2,6},{3,7},{4,0},{5,1},{6,2},{7,3},{8,12},{9,13},{10,... | collective-permute-start | bytes 1081352 | tf_op jit(solution)/shard_map/ppermute | solution.py:290
  135.2 32.2 %collective-permute-start.23 = (bf16[4,176,256]{2,1,0:T(8,128)(2,1)}, bf16[4,176,256]{2,1,0:T(8,128)(2,1)S(1)}, u32[]{:S(2)}, u32[]{:S(2)}) collective-permute-start(bf16[4,176,256]{2,1,0:T(8,128)(2,1)} %get-tuple-element.133), channel_id=1, source_target_pairs={{0,6},{1,7},{2,4},{3,5},{4,2},{5,3},{6,0},{7,1},{8,14},{9,15},{10,... | collective-permute-start | bytes 1081352 | tf_op jit(solution)/shard_map/ppermute | solution.py:290
  143.6 25.0 %collective-permute-start.24 = (bf16[4,176,256]{2,1,0:T(8,128)(2,1)}, bf16[4,176,256]{2,1,0:T(8,128)(2,1)S(1)}, u32[]{:S(2)}, u32[]{:S(2)}) collective-permute-start(bf16[4,176,256]{2,1,0:T(8,128)(2,1)} %get-tuple-element.134), channel_id=1, source_target_pairs={{0,3},{1,2},{2,1},{3,0},{4,7},{5,6},{6,5},{7,4},{8,11},{9,10},{10,... | collective-permute-start | bytes 1081352 | tf_op jit(solution)/shard_map/ppermute | solution.py:290
  144.6 25.1 %collective-permute-start.25 = (bf16[4,176,256]{2,1,0:T(8,128)(2,1)}, bf16[4,176,256]{2,1,0:T(8,128)(2,1)S(1)}, u32[]{:S(2)}, u32[]{:S(2)}) collective-permute-start(bf16[4,176,256]{2,1,0:T(8,128)(2,1)} %get-tuple-element.135), channel_id=1, source_target_pairs={{0,5},{1,4},{2,7},{3,6},{4,1},{5,0},{6,3},{7,2},{8,13},{9,12},{10,... | collective-permute-start | bytes 1081352 | tf_op jit(solution)/shard_map/ppermute | solution.py:290
  150.4 24.0 %collective-permute-start.26 = (bf16[4,176,256]{2,1,0:T(8,128)(2,1)}, bf16[4,176,256]{2,1,0:T(8,128)(2,1)}, u32[]{:S(2)}, u32[]{:S(2)}) collective-permute-start(bf16[4,176,256]{2,1,0:T(8,128)(2,1)} %get-tuple-element.136), channel_id=1, source_target_pairs={{0,7},{1,6},{2,5},{3,4},{4,3},{5,2},{6,1},{7,0},{8,15},{9,14},{10,... | collective-permute-start | bytes 1081352 | tf_op jit(solution)/shard_map/ppermute | solution.py:290
  166.1 17.2 %collective-permute-start.35 = (bf16[5,176,256]{2,1,0:T(8,128)(2,1)}, bf16[5,176,256]{2,1,0:T(8,128)(2,1)S(1)}, u32[]{:S(2)}, u32[]{:S(2)}) collective-permute-start(bf16[5,176,256]{2,1,0:T(8,128)(2,1)} %get-tuple-element.152), channel_id=1, source_target_pairs={{0,2},{1,3},{2,0},{3,1},{4,6},{5,7},{6,4},{7,5},{8,10},{9,11},{10,... | collective-permute-start | bytes 1351688 | tf_op jit(solution)/shard_map/ppermute | solution.py:290
  168.6 25.6 %collective-permute-start.36 = (bf16[5,176,256]{2,1,0:T(8,128)(2,1)}, bf16[5,176,256]{2,1,0:T(8,128)(2,1)S(1)}, u32[]{:S(2)}, u32[]{:S(2)}) collective-permute-start(bf16[5,176,256]{2,1,0:T(8,128)(2,1)} %get-tuple-element.153), channel_id=1, source_target_pairs={{0,4},{1,5},{2,6},{3,7},{4,0},{5,1},{6,2},{7,3},{8,12},{9,13},{10,... | collective-permute-start | bytes 1351688 | tf_op jit(solution)/shard_map/ppermute | solution.py:290
  169.7 32.1 %collective-permute-start.37 = (bf16[5,176,256]{2,1,0:T(8,128)(2,1)}, bf16[5,176,256]{2,1,0:T(8,128)(2,1)S(1)}, u32[]{:S(2)}, u32[]{:S(2)}) collective-permute-start(bf16[5,176,256]{2,1,0:T(8,128)(2,1)} %get-tuple-element.154), channel_id=1, source_target_pairs={{0,6},{1,7},{2,4},{3,5},{4,2},{5,3},{6,0},{7,1},{8,14},{9,15},{10,... | collective-permute-start | bytes 1351688 | tf_op jit(solution)/shard_map/ppermute | solution.py:290
  174.4 29.2 %collective-permute-start.38 = (bf16[5,176,256]{2,1,0:T(8,128)(2,1)}, bf16[5,176,256]{2,1,0:T(8,128)(2,1)S(1)}, u32[]{:S(2)}, u32[]{:S(2)}) collective-permute-start(bf16[5,176,256]{2,1,0:T(8,128)(2,1)} %get-tuple-element.155), channel_id=1, source_target_pairs={{0,3},{1,2},{2,1},{3,0},{4,7},{5,6},{6,5},{7,4},{8,11},{9,10},{10,... | collective-permute-start | bytes 1351688 | tf_op jit(solution)/shard_map/ppermute | solution.py:290
  175.5 28.5 %collective-permute-start.39 = (bf16[5,176,256]{2,1,0:T(8,128)(2,1)}, bf16[5,176,256]{2,1,0:T(8,128)(2,1)S(1)}, u32[]{:S(2)}, u32[]{:S(2)}) collective-permute-start(bf16[5,176,256]{2,1,0:T(8,128)(2,1)} %get-tuple-element.156), channel_id=1, source_target_pairs={{0,5},{1,4},{2,7},{3,6},{4,1},{5,0},{6,3},{7,2},{8,13},{9,12},{10,... | collective-permute-start | bytes 1351688 | tf_op jit(solution)/shard_map/ppermute | solution.py:290
  183.3 29.6 %collective-permute-start.40 = (bf16[5,176,256]{2,1,0:T(8,128)(2,1)}, bf16[5,176,256]{2,1,0:T(8,128)(2,1)S(1)}, u32[]{:S(2)}, u32[]{:S(2)}) collective-permute-start(bf16[5,176,256]{2,1,0:T(8,128)(2,1)} %get-tuple-element.157), channel_id=1, source_target_pairs={{0,7},{1,6},{2,5},{3,4},{4,3},{5,2},{6,1},{7,0},{8,15},{9,14},{10,... | collective-permute-start | bytes 1351688 | tf_op jit(solution)/shard_map/ppermute | solution.py:290
  194.2 19.9 %collective-permute-start.41 = (bf16[5,176,256]{2,1,0:T(8,128)(2,1)}, bf16[5,176,256]{2,1,0:T(8,128)(2,1)S(1)}, u32[]{:S(2)}, u32[]{:S(2)}) collective-permute-start(bf16[5,176,256]{2,1,0:T(8,128)(2,1)} %get-tuple-element.158), channel_id=1, source_target_pairs={{0,1},{1,0},{2,3},{3,2},{4,5},{5,4},{6,7},{7,6},{8,9},{9,8},{10,11... | collective-permute-start | bytes 1351688 | tf_op jit(solution)/shard_map/ppermute | solution.py:290
  201.8 20.2 %collective-permute-start.52 = (bf16[5,176,256]{2,1,0:T(8,128)(2,1)}, bf16[5,176,256]{2,1,0:T(8,128)(2,1)S(1)}, u32[]{:S(2)}, u32[]{:S(2)}) collective-permute-start(bf16[5,176,256]{2,1,0:T(8,128)(2,1)} %get-tuple-element.170), channel_id=1, source_target_pairs={{0,2},{1,3},{2,0},{3,1},{4,6},{5,7},{6,4},{7,5},{8,10},{9,11},{10,... | collective-permute-start | bytes 1351688 | tf_op jit(solution)/shard_map/ppermute | solution.py:290
  203.6 28.9 %collective-permute-start.53 = (bf16[5,176,256]{2,1,0:T(8,128)(2,1)}, bf16[5,176,256]{2,1,0:T(8,128)(2,1)S(1)}, u32[]{:S(2)}, u32[]{:S(2)}) collective-permute-start(bf16[5,176,256]{2,1,0:T(8,128)(2,1)} %get-tuple-element.171), channel_id=1, source_target_pairs={{0,4},{1,5},{2,6},{3,7},{4,0},{5,1},{6,2},{7,3},{8,12},{9,13},{10,... | collective-permute-start | bytes 1351688 | tf_op jit(solution)/shard_map/ppermute | solution.py:290
  204.0 39.4 %collective-permute-start.54 = (bf16[5,176,256]{2,1,0:T(8,128)(2,1)}, bf16[5,176,256]{2,1,0:T(8,128)(2,1)}, u32[]{:S(2)}, u32[]{:S(2)}) collective-permute-start(bf16[5,176,256]{2,1,0:T(8,128)(2,1)} %get-tuple-element.172), channel_id=1, source_target_pairs={{0,6},{1,7},{2,4},{3,5},{4,2},{5,3},{6,0},{7,1},{8,14},{9,15},{10,... | collective-permute-start | bytes 1351688 | tf_op jit(solution)/shard_map/ppermute | solution.py:290
  212.9 32.1 %collective-permute-start.55 = (bf16[5,176,256]{2,1,0:T(8,128)(2,1)}, bf16[5,176,256]{2,1,0:T(8,128)(2,1)}, u32[]{:S(2)}, u32[]{:S(2)}) collective-permute-start(bf16[5,176,256]{2,1,0:T(8,128)(2,1)} %get-tuple-element.173), channel_id=1, source_target_pairs={{0,3},{1,2},{2,1},{3,0},{4,7},{5,6},{6,5},{7,4},{8,11},{9,10},{10,... | collective-permute-start | bytes 1351688 | tf_op jit(solution)/shard_map/ppermute | solution.py:290
  214.1 30.9 %collective-permute-start.56 = (bf16[5,176,256]{2,1,0:T(8,128)(2,1)}, bf16[5,176,256]{2,1,0:T(8,128)(2,1)}, u32[]{:S(2)}, u32[]{:S(2)}) collective-permute-start(bf16[5,176,256]{2,1,0:T(8,128)(2,1)} %get-tuple-element.174), channel_id=1, source_target_pairs={{0,5},{1,4},{2,7},{3,6},{4,1},{5,0},{6,3},{7,2},{8,13},{9,12},{10,... | collective-permute-start | bytes 1351688 | tf_op jit(solution)/shard_map/ppermute | solution.py:290
  222.0 29.3 %collective-permute-start.57 = (bf16[5,176,256]{2,1,0:T(8,128)(2,1)}, bf16[5,176,256]{2,1,0:T(8,128)(2,1)}, u32[]{:S(2)}, u32[]{:S(2)}) collective-permute-start(bf16[5,176,256]{2,1,0:T(8,128)(2,1)} %get-tuple-element.175), channel_id=1, source_target_pairs={{0,7},{1,6},{2,5},{3,4},{4,3},{5,2},{6,1},{7,0},{8,15},{9,14},{10,... | collective-permute-start | bytes 1351688 | tf_op jit(solution)/shard_map/ppermute | solution.py:290
  232.5 20.1 %collective-permute-start.58 = (bf16[5,176,256]{2,1,0:T(8,128)(2,1)}, bf16[5,176,256]{2,1,0:T(8,128)(2,1)}, u32[]{:S(2)}, u32[]{:S(2)}) collective-permute-start(bf16[5,176,256]{2,1,0:T(8,128)(2,1)} %get-tuple-element.176), channel_id=1, source_target_pairs={{0,1},{1,0},{2,3},{3,2},{4,5},{5,4},{6,7},{7,6},{8,9},{9,8},{10,11... | collective-permute-start | bytes 1351688 | tf_op jit(solution)/shard_map/ppermute | solution.py:290
  245.0 18.2 %collective-permute-start.43 = (bf16[3,176,256]{2,1,0:T(8,128)(2,1)}, bf16[3,176,256]{2,1,0:T(8,128)(2,1)S(1)}, u32[]{:S(2)}, u32[]{:S(2)}) collective-permute-start(bf16[3,176,256]{2,1,0:T(8,128)(2,1)} %get-tuple-element.161), channel_id=1, source_target_pairs={{0,4},{1,5},{2,6},{3,7},{4,0},{5,1},{6,2},{7,3},{8,12},{9,13},{10,... | collective-permute-start | bytes 811016 | tf_op jit(solution)/shard_map/ppermute | solution.py:290
  245.0 28.5 %collective-permute-start.44 = (bf16[3,176,256]{2,1,0:T(8,128)(2,1)}, bf16[3,176,256]{2,1,0:T(8,128)(2,1)S(1)}, u32[]{:S(2)}, u32[]{:S(2)}) collective-permute-start(bf16[3,176,256]{2,1,0:T(8,128)(2,1)} %get-tuple-element.162), channel_id=1, source_target_pairs={{0,6},{1,7},{2,4},{3,5},{4,2},{5,3},{6,0},{7,1},{8,14},{9,15},{10,... | collective-permute-start | bytes 811016 | tf_op jit(solution)/shard_map/ppermute | solution.py:290
  251.3 24.0 %collective-permute-start.45 = (bf16[3,176,256]{2,1,0:T(8,128)(2,1)}, bf16[3,176,256]{2,1,0:T(8,128)(2,1)S(1)}, u32[]{:S(2)}, u32[]{:S(2)}) collective-permute-start(bf16[3,176,256]{2,1,0:T(8,128)(2,1)} %get-tuple-element.163), channel_id=1, source_target_pairs={{0,3},{1,2},{2,1},{3,0},{4,7},{5,6},{6,5},{7,4},{8,11},{9,10},{10,... | collective-permute-start | bytes 811016 | tf_op jit(solution)/shard_map/ppermute | solution.py:290
  252.7 22.6 %collective-permute-start.46 = (bf16[3,176,256]{2,1,0:T(8,128)(2,1)}, bf16[3,176,256]{2,1,0:T(8,128)(2,1)S(1)}, u32[]{:S(2)}, u32[]{:S(2)}) collective-permute-start(bf16[3,176,256]{2,1,0:T(8,128)(2,1)} %get-tuple-element.164), channel_id=1, source_target_pairs={{0,5},{1,4},{2,7},{3,6},{4,1},{5,0},{6,3},{7,2},{8,13},{9,12},{10,... | collective-permute-start | bytes 811016 | tf_op jit(solution)/shard_map/ppermute | solution.py:290
  256.8 20.2 %collective-permute-start.47 = (bf16[3,176,256]{2,1,0:T(8,128)(2,1)}, bf16[3,176,256]{2,1,0:T(8,128)(2,1)S(1)}, u32[]{:S(2)}, u32[]{:S(2)}) collective-permute-start(bf16[3,176,256]{2,1,0:T(8,128)(2,1)} %get-tuple-element.165), channel_id=1, source_target_pairs={{0,7},{1,6},{2,5},{3,4},{4,3},{5,2},{6,1},{7,0},{8,15},{9,14},{10,... | collective-permute-start | bytes 811016 | tf_op jit(solution)/shard_map/ppermute | solution.py:290
  263.2 14.5 %collective-permute-start.48 = (bf16[3,176,256]{2,1,0:T(8,128)(2,1)}, bf16[3,176,256]{2,1,0:T(8,128)(2,1)S(1)}, u32[]{:S(2)}, u32[]{:S(2)}) collective-permute-start(bf16[3,176,256]{2,1,0:T(8,128)(2,1)} %get-tuple-element.166), channel_id=1, source_target_pairs={{0,1},{1,0},{2,3},{3,2},{4,5},{5,4},{6,7},{7,6},{8,9},{9,8},{10,11... | collective-permute-start | bytes 811016 | tf_op jit(solution)/shard_map/ppermute | solution.py:290
  275.3 21.8 %collective-permute-start.68 = (bf16[2,176,256]{2,1,0:T(8,128)(2,1)}, bf16[2,176,256]{2,1,0:T(8,128)(2,1)S(1)}, u32[]{:S(2)}, u32[]{:S(2)}) collective-permute-start(bf16[2,176,256]{2,1,0:T(8,128)(2,1)} %get-tuple-element.192), channel_id=1, source_target_pairs={{0,6},{1,7},{2,4},{3,5},{4,2},{5,3},{6,0},{7,1},{8,14},{9,15},{10,... | collective-permute-start | bytes 540680 | tf_op jit(solution)/shard_map/ppermute | solution.py:290
  277.0 20.1 %collective-permute-start.69 = (bf16[2,176,256]{2,1,0:T(8,128)(2,1)}, bf16[2,176,256]{2,1,0:T(8,128)(2,1)S(1)}, u32[]{:S(2)}, u32[]{:S(2)}) collective-permute-start(bf16[2,176,256]{2,1,0:T(8,128)(2,1)} %get-tuple-element.193), channel_id=1, source_target_pairs={{0,3},{1,2},{2,1},{3,0},{4,7},{5,6},{6,5},{7,4},{8,11},{9,10},{10,... | collective-permute-start | bytes 540680 | tf_op jit(solution)/shard_map/ppermute | solution.py:290
  277.6 19.6 %collective-permute-start.70 = (bf16[2,176,256]{2,1,0:T(8,128)(2,1)}, bf16[2,176,256]{2,1,0:T(8,128)(2,1)S(1)}, u32[]{:S(2)}, u32[]{:S(2)}) collective-permute-start(bf16[2,176,256]{2,1,0:T(8,128)(2,1)} %get-tuple-element.194), channel_id=1, source_target_pairs={{0,5},{1,4},{2,7},{3,6},{4,1},{5,0},{6,3},{7,2},{8,13},{9,12},{10,... | collective-permute-start | bytes 540680 | tf_op jit(solution)/shard_map/ppermute | solution.py:290
  281.2 19.5 %collective-permute-start.71 = (bf16[2,176,256]{2,1,0:T(8,128)(2,1)}, bf16[2,176,256]{2,1,0:T(8,128)(2,1)S(1)}, u32[]{:S(2)}, u32[]{:S(2)}) collective-permute-start(bf16[2,176,256]{2,1,0:T(8,128)(2,1)} %get-tuple-element.195), channel_id=1, source_target_pairs={{0,7},{1,6},{2,5},{3,4},{4,3},{5,2},{6,1},{7,0},{8,15},{9,14},{10,... | collective-permute-start | bytes 540680 | tf_op jit(solution)/shard_map/ppermute | solution.py:290
  297.3 15.2 %collective-permute-start.64 = (bf16[1,176,256]{2,1,0:T(8,128)(2,1)}, bf16[1,176,256]{2,1,0:T(8,128)(2,1)S(1)}, u32[]{:S(2)}, u32[]{:S(2)}) collective-permute-start(bf16[1,176,256]{2,1,0:T(8,128)(2,1)} %get-tuple-element.186), channel_id=1, source_target_pairs={{0,6},{1,7},{2,4},{3,5},{4,2},{5,3},{6,0},{7,1},{8,14},{9,15},{10,... | collective-permute-start | bytes 270344 | tf_op jit(solution)/shard_map/ppermute | solution.py:290
  300.7 13.5 %collective-permute-start.59 = (bf16[1,176,256]{2,1,0:T(8,128)(2,1)}, bf16[1,176,256]{2,1,0:T(8,128)(2,1)S(1)}, u32[]{:S(2)}, u32[]{:S(2)}) collective-permute-start(bf16[1,176,256]{2,1,0:T(8,128)(2,1)} %get-tuple-element.180), channel_id=1, source_target_pairs={{0,3},{1,2},{2,1},{3,0},{4,7},{5,6},{6,5},{7,4},{8,11},{9,10},{10,... | collective-permute-start | bytes 270344 | tf_op jit(solution)/shard_map/ppermute | solution.py:290
  (88 other events, 1121.3 us)
